TPU v7x, 128 devices: a whole 4x4x4 slice. The times are simulated.
128 devices in a mesh: row: 8 (over y, z_lo), col: 16 (over x, z_hi, core).
Axes of the slice: x: 4, y: 4, z: 4 (z_hi: 2, z_lo: 2; z = z_hi * 2 + z_lo), core: 2. Of those that a mesh axis runs over, the one named last changes fastest.
Arguments:
- object_field: float32 [2, 2048, 4096], P(None, 'row', 'col'), may hold values from -40 to 40
- probe: float32 [2, 4, 256, 256], replicated, may hold values from -3 to 3
- pos_rows: int32 [8, 16, 2, 3], P('row', 'col'), may hold values from 0 to 255
- pos_cols: int32 [8, 16, 2, 3], P('row', 'col'), may hold values from 0 to 255
- counts: int32 [8, 16, 2], P('row', 'col'), may hold values from 1 to 3, as said below
- magnitudes: float32 [8, 16, 2, 3, 256, 256], P('row', 'col'), may hold values from 0 to 4
Outputs:
- object_out: float32 [2, 2048, 4096], P(None, 'row', 'col')
- probe_out: float32 [2, 4, 256, 256], replicated
- errors: float32 [4], replicated
Inputs may be any that keep to these rules, and one draw needn't show every extreme that they name: `counts`: every tile holds at least one live position in each batch, and in every batch some tile holds 3.
All inputs are finite; a program needn't handle non-finite values.
Results may differ from a plain program's by a relative error of at most 0.0015.
Values sent between devices are 32-bit elements; how exact they have to be, the bound alone decides.
A program may use at most 128 MiB of HBM per device.

v0:
```python
import functools
import math

import jax
import jax.numpy as jnp
from jax import lax
from jax.sharding import Mesh
from jax.sharding import PartitionSpec as P

BATCHES = 2
ITERS = 2
ROW = ("row_0", "row_1")
COL = ("col_0", "col_1", "col_2")
ROW_COL = ("row_0", "row_1", "col_0", "col_1", "col_2")


object_rate = 0.9
probe_rate = 0.5
floor_value = 0.5
tiny_value = 1e-06


def shifted(value, axis, steps):
    count = lax.axis_size(axis)
    leading, last = (max(0, -steps), min(count, count - steps))
    return lax.ppermute(value, axis, [(source, source + steps) for source in range(leading, last)])


def padded(array, sides, width):
    for axis, dim in sides:
        devices, length = (lax.axis_size(axis), array.shape[dim])
        up = [(i, (i + 1) % devices) for i in range(devices - 1)]
        down = [(j, i) for i, j in up]
        last = lax.slice_in_dim(array, length - width, length, axis=dim)
        leading = lax.slice_in_dim(array, 0, width, axis=dim)
        before = lax.ppermute(last, axis, up)
        after = lax.ppermute(leading, axis, down)
        array = jnp.concatenate([before, array, after], axis=dim)
    return array


def over_axes(array, axes):
    return functools.reduce(lax.psum, axes, array)


def dft_tables(probe_side):
    indices = jnp.arange(probe_side, dtype=jnp.int32)
    phase_index = indices[:, None] * indices[None, :] % probe_side
    angles = phase_index.astype(jnp.float32) * (2.0 * math.pi / probe_side)
    norm_scale = 1.0 / math.sqrt(probe_side)
    cosine = jnp.cos(angles) * norm_scale
    sine_part = -jnp.sin(angles) * norm_scale
    forward = jnp.stack([jnp.stack([cosine, -sine_part]), jnp.stack([sine_part, cosine])]).astype(
        jnp.bfloat16
    )
    inverse = jnp.stack([jnp.stack([cosine, sine_part]), jnp.stack([-sine_part, cosine])]).astype(
        jnp.bfloat16
    )
    return (forward, inverse)


def transform(field, table):
    left_half = jnp.einsum(
        "oixa,imab->omxb", table, field, preferred_element_type=jnp.float32
    ).astype(jnp.bfloat16)
    return jnp.einsum("imxb,oiby->omxy", left_half, table, preferred_element_type=jnp.float32)


def position_terms(window, probe, amplitude, forward, inverse):
    probe_re = probe[0]
    probe_im = probe[1]
    window_re = window[0][None]
    window_im = window[1][None]
    exit_wave = jnp.stack(
        [probe_re * window_re - probe_im * window_im, probe_re * window_im + probe_im * window_re]
    ).astype(jnp.bfloat16)
    far_field = transform(exit_wave, forward)
    modulus = jnp.sqrt(jnp.sum(far_field * far_field, axis=(0, 1)))
    factor = amplitude / jnp.maximum(modulus, floor_value) - 1.0
    correction = (far_field * factor[None, None]).astype(jnp.bfloat16)
    update_wave = transform(correction, inverse)
    wave_re = update_wave[0]
    wave_im = update_wave[1]
    object_term = jnp.stack(
        [
            jnp.sum(probe_re * wave_re + probe_im * wave_im, axis=0),
            jnp.sum(probe_re * wave_im - probe_im * wave_re, axis=0),
        ]
    )
    probe_term = jnp.stack(
        [window_re * wave_re + window_im * wave_im, window_re * wave_im - window_im * wave_re]
    )
    power_term = jnp.sum(window * window)
    misfit = jnp.sum(jnp.square(modulus - amplitude))
    return (object_term, probe_term, power_term, misfit)


def return_rims(object_grad, margin):
    from_above = shifted(object_grad[:, -margin:, :], ROW, 1)
    from_below = shifted(object_grad[:, :margin, :], ROW, -1)
    middle = object_grad[:, margin:-margin, :]
    middle = middle.at[:, :margin, :].add(from_above)
    middle = middle.at[:, -margin:, :].add(from_below)
    from_left = shifted(middle[:, :, -margin:], COL, 1)
    from_right = shifted(middle[:, :, :margin], COL, -1)
    interior = middle[:, :, margin:-margin]
    interior = interior.at[:, :, :margin].add(from_left)
    interior = interior.at[:, :, -margin:].add(from_right)
    return interior


def on_device(object_field, probe, pos_rows, pos_cols, counts, magnitudes):
    probe_side = probe.shape[2]
    margin = probe_side // 2
    forward, inverse = dft_tables(probe_side)
    errors = []
    for sweep in range(ITERS):
        for batch in range(BATCHES):
            extended = padded(object_field, ((ROW, 1), (COL, 2)), margin)
            live_count = counts[0, 0, batch]

            def window_at(slot_index):
                anchor = (
                    jnp.int32(0),
                    pos_rows[0, 0, batch, slot_index],
                    pos_cols[0, 0, batch, slot_index],
                )
                return (anchor, lax.dynamic_slice(extended, anchor, (2, probe_side, probe_side)))

            def visit(slot_index, carry):
                object_grad, probe_grad, power_sum, misfit_sum = carry
                anchor, window = window_at(slot_index)
                amplitude = magnitudes[0, 0, batch, slot_index]
                object_term, probe_term, power_term, misfit = position_terms(
                    window, probe, amplitude, forward, inverse
                )
                region = lax.dynamic_slice(object_grad, anchor, (2, probe_side, probe_side))
                object_grad = lax.dynamic_update_slice(object_grad, region + object_term, anchor)
                return (
                    object_grad,
                    probe_grad + probe_term,
                    power_sum + power_term,
                    misfit_sum + misfit,
                )

            start = (
                jnp.zeros(extended.shape, jnp.float32),
                jnp.zeros(probe.shape, jnp.float32),
                jnp.float32(0.0),
                jnp.float32(0.0),
            )
            object_grad, probe_grad, power_sum, misfit_sum = lax.fori_loop(
                0, live_count, visit, start
            )
            interior = return_rims(object_grad, margin)
            probe_peak = jnp.max(jnp.sum(probe * probe, axis=(0, 1))) + tiny_value
            new_object = object_field + object_rate / probe_peak * interior
            summed, power_total = lax.psum((probe_grad, power_sum), ROW_COL)
            probe = probe + probe_rate * probe_side * probe_side / power_total * summed
            object_field = new_object
            errors.append(misfit_sum)
    totals = over_axes(jnp.stack(errors), ROW_COL)
    return (object_field, probe, totals)


def solution(mesh):
    finer = Mesh(mesh.devices.reshape(4, 2, 4, 2, 2), ("row_0", "row_1", "col_0", "col_1", "col_2"))
    return jax.shard_map(
        on_device,
        mesh=finer,
        in_specs=(
            P(None, ROW, COL),
            P(),
            P(ROW, COL, None, None),
            P(ROW, COL, None, None),
            P(ROW, COL, None),
            P(ROW, COL, None, None, None, None),
        ),
        out_specs=(P(None, ROW, COL), P(), P()),
        check_vma=False,
    )
```

profile of v0, /device:TPU:1, one launch (start us, length us, event | category | flops | bytes accessed | tf_op | source)
XLA Modules:
  0.0 1256.1 jit_solution(9451795665652992884)
XLA Ops:
  15.0 8.1 collective-permute-done
  25.3 6.8 collective-permute-start.2
  50.2 33.2 %while.88 = (s32[]{:T(128)}, f32[2,512,512]{2,1,0:T(8,128)}, f32[2,4,256,256]{3,2,0,1:T(8,128)}, f32[]{:T(128)}, f32[]{:T(128)}, /*index=5*/s32[]{:T(128)}, s32[...) while((s32[]{:T(128)}, f32[2,512,512]{2,1,0:T(8,128)}, ...), condition=%wide.region_8.9_spmd, body=%wide.region_2.8_spmd.sunk | while | flops 2160263168 | bytes 47972772 | solution.py:152
  85.9 36.6 %collective-permute-start.4 = (f32[2,128,512]{2,1,0:T(8,128)}, f32[2,128,512]{2,1,0:T(8,128)}, u32[]{:S(2)}, u32[]{:S(2)}) collective-permute-start(f32[2,128,512]{2,1,0:T(8,128)} %get-tuple-element.1165), channel_id=1, source_target_pairs={{0,16},{16,32},{32,48},{48,64},{64,80},{80,96},{96,112},{1,17},{17... | collective-permute-start | bytes 1572872 | tf_op jit(solution)/shard_map/ppermute | solution.py:26
  125.5 8.3 collective-permute-done.4
  136.9 39.5 %collective-permute-start.6 = (f32[2,256,128]{2,1,0:T(8,128)}, f32[2,256,128]{2,1,0:T(8,128)}, u32[]{:S(2)}, u32[]{:S(2)}) collective-permute-start(f32[2,256,128]{2,1,0:T(8,128)} %get-tuple-element.1179), channel_id=1, source_target_pairs={{0,1},{1,2},{2,3},{3,4},{4,5},{5,6},{6,7},{7,8},{8,9},{9,10},{10,1... | collective-permute-start | bytes 786440 | tf_op jit(solution)/shard_map/ppermute | solution.py:26
  178.4 75.3 %psum.91 = f32[]{:T(128)} all-reduce(f32[]{:T(128)} %get-tuple-element.864), channel_id=1, replica_groups=mesh['row_0'=4,'row_1'=2,'col_0'=4,'col_1'=2,'col_2'=2] {'row_0','row_1'..., use_global_device_ids=true, to_apply=%region_9.10 | all-reduce | flops 1 | bytes 8 | tf_op jit(solution)/shard_map/psum | solution.py:158
  258.6 57.5 %all-reduce.5.cloned.1.call-done = f32[2,4,256,256]{3,2,1,0:T(8,128)} async-done(((f32[2,4,256,256]{3,2,1,0:T(8,128)}), f32[2,4,256,256]{3,2,1,0:T(8,128)}) %all-reduce.5.cloned.1.call-update) | async-done | bytes 2097168 | tf_op jit(solution)/shard_map/psum | solution.py:158
  334.0 8.8 collective-permute-start.10
  346.6 8.3 collective-permute-done.10
  361.0 65.8 %while.89 = (s32[]{:T(128)}, f32[2,512,512]{2,1,0:T(8,128)}, f32[2,4,256,256]{3,2,0,1:T(8,128)}, f32[]{:T(128)}, f32[]{:T(128)}, /*index=5*/s32[]{:T(128)}, s32[...) while((s32[]{:T(128)}, f32[2,512,512]{2,1,0:T(8,128)}, ...), condition=%wide.region_19.20_spmd, body=%wide.region_13.19_spmd.sunk | while | flops 2160263168 | bytes 47972772 | solution.py:152
  418.2 6.8 dynamic_update_slice.29
  431.0 9.5 collective-permute-done.12
  441.6 10.2 collective-permute-start.14
  457.9 25.5 %collective-permute-done.15 = f32[2,256,128]{2,1,0:T(8,128)} collective-permute-done((f32[2,256,128]{2,1,0:T(8,128)}, f32[2,256,128]{2,1,0:T(8,128)}, u32[]{:S(2)}, u32[]{:S(2)}) %collective-permute-start.15) | collective-permute-done | bytes 262176 | tf_op jit(solution)/shard_map/ppermute | solution.py:26
  489.1 8.5 collective-permute-done.17
  498.7 11.3 collective-permute-start.18
  511.9 90.5 %psum.93 = f32[]{:T(128)} all-reduce(f32[]{:T(128)} %get-tuple-element.867), channel_id=1, replica_groups=mesh['row_0'=4,'row_1'=2,'col_0'=4,'col_1'=2,'col_2'=2] {'row_0','row_1'..., use_global_device_ids=true, to_apply=%region_20.21 | all-reduce | flops 1 | bytes 8 | tf_op jit(solution)/shard_map/psum | solution.py:158
  603.2 62.0 %all-reduce.7.cloned.1.call-done = f32[2,4,256,256]{3,2,1,0:T(8,128)} async-done(((f32[2,4,256,256]{3,2,1,0:T(8,128)}), f32[2,4,256,256]{3,2,1,0:T(8,128)}) %all-reduce.7.cloned.1.call-update) | async-done | bytes 2097168 | tf_op jit(solution)/shard_map/psum | solution.py:158
  675.0 32.7 %while.90 = (s32[]{:T(128)}, f32[2,512,512]{2,1,0:T(8,128)}, f32[2,4,256,256]{3,2,0,1:T(8,128)}, f32[]{:T(128)}, f32[]{:T(128)}, /*index=5*/s32[]{:T(128)}, s32[...) while((s32[]{:T(128)}, f32[2,512,512]{2,1,0:T(8,128)}, ...), condition=%wide.region_30.31_spmd, body=%wide.region_24.30_spmd.sunk | while | flops 2160263168 | bytes 47972772 | solution.py:152
  709.1 33.8 %collective-permute-start.20 = (f32[2,128,512]{2,1,0:T(8,128)S(1)}, f32[2,128,512]{2,1,0:T(8,128)S(1)}, u32[]{:S(2)}, u32[]{:S(2)}) collective-permute-start(f32[2,128,512]{2,1,0:T(8,128)S(1)} %get-tuple-element.1160), channel_id=1, source_target_pairs={{0,16},{16,32},{32,48},{48,64},{64,80},{80,96},{96,112},{1,17},{17... | collective-permute-start | bytes 1572872 | tf_op jit(solution)/shard_map/ppermute | solution.py:26
  744.4 13.9 %collective-permute-done.20 = f32[2,128,512]{2,1,0:T(8,128)S(1)} collective-permute-done((f32[2,128,512]{2,1,0:T(8,128)S(1)}, f32[2,128,512]{2,1,0:T(8,128)S(1)}, u32[]{:S(2)}, u32[]{:S(2)}) %collective-permute-start.20) | collective-permute-done | bytes 524320 | tf_op jit(solution)/shard_map/ppermute | solution.py:26
  759.4 33.5 %collective-permute-start.22 = (f32[2,256,128]{2,1,0:T(8,128)}, f32[2,256,128]{2,1,0:T(8,128)}, u32[]{:S(2)}, u32[]{:S(2)}) collective-permute-start(f32[2,256,128]{2,1,0:T(8,128)} %get-tuple-element.1171), channel_id=1, source_target_pairs={{0,1},{1,2},{2,3},{3,4},{4,5},{5,6},{6,7},{7,8},{8,9},{9,10},{10,1... | collective-permute-start | bytes 786440 | tf_op jit(solution)/shard_map/ppermute | solution.py:26
  824.3 84.1 %psum.95 = f32[]{:T(128)} all-reduce(f32[]{:T(128)} %get-tuple-element.870), channel_id=1, replica_groups=mesh['row_0'=4,'row_1'=2,'col_0'=4,'col_1'=2,'col_2'=2] {'row_0','row_1'..., use_global_device_ids=true, to_apply=%region_31.32 | all-reduce | flops 1 | bytes 8 | tf_op jit(solution)/shard_map/psum | solution.py:158
  909.1 63.5 %all-reduce.9.cloned.1.call-done = f32[2,4,256,256]{3,2,1,0:T(8,128)} async-done(((f32[2,4,256,256]{3,2,1,0:T(8,128)}), f32[2,4,256,256]{3,2,1,0:T(8,128)}) %all-reduce.9.cloned.1.call-update) | async-done | bytes 2097168 | tf_op jit(solution)/shard_map/psum | solution.py:158
  982.4 65.6 %while.91 = (s32[]{:T(128)}, f32[2,512,512]{2,1,0:T(8,128)}, f32[2,4,256,256]{3,2,0,1:T(8,128)}, f32[]{:T(128)}, f32[]{:T(128)}, /*index=5*/s32[]{:T(128)}, s32[...) while((s32[]{:T(128)}, f32[2,512,512]{2,1,0:T(8,128)}, ...), condition=%wide.region_41.42_spmd, body=%wide.region_35.41_spmd.sunk | while | flops 2160263168 | bytes 47972772 | solution.py:152
  1039.5 6.7 dynamic_update_slice.31
  1076.7 39.3 %psum.99 = f32[4]{0:T(128)S(1)} all-reduce(f32[4]{0:T(128)S(1)} %pad_maximum_fusion.13), channel_id=1, replica_groups=mesh['row_0'=4,'row_1'=2,'col_0'=4,'col_1'=2,'col_2'=2] {'row_0'}, use_global_device_ids=true, to_apply=%region_44.45 | all-reduce | flops 4 | bytes 32 | tf_op jit(solution)/shard_map/psum | solution.py:43
  1121.1 18.2 %psum.101 = f32[4]{0:T(128)S(1)} all-reduce(f32[4]{0:T(128)S(1)} %psum.100), channel_id=1, replica_groups=mesh['row_0'=4,'row_1'=2,'col_0'=4,'col_1'=2,'col_2'=2] {'col_0'}, use_global_device_ids=true, to_apply=%region_46.47 | all-reduce | flops 4 | bytes 32 | tf_op jit(solution)/shard_map/psum | solution.py:43
  1139.3 6.6 psum.102
  1145.9 71.1 %psum.97 = f32[]{:T(128)} all-reduce(f32[]{:T(128)} %get-tuple-element.873), channel_id=1, replica_groups=mesh['row_0'=4,'row_1'=2,'col_0'=4,'col_1'=2,'col_2'=2] {'row_0','row_1'..., use_global_device_ids=true, to_apply=%region_42.43 | all-reduce | flops 1 | bytes 8 | tf_op jit(solution)/shard_map/psum | solution.py:158
  1224.0 22.0 %all-reduce.11.cloned.1.call-done = f32[2,4,256,256]{3,2,1,0:T(8,128)} async-done(((f32[2,4,256,256]{3,2,1,0:T(8,128)}), f32[2,4,256,256]{3,2,1,0:T(8,128)}) %all-reduce.11.cloned.1.call-update) | async-done | bytes 2097168 | tf_op jit(solution)/shard_map/psum | solution.py:158
  (286 shorter events, 333.5 us)
Async XLA Ops:
  7.2 309.0 %all-reduce.5.cloned.1.call-start = ((), (), s32[]{:S(2)}) async-start(), calls=%async_computation | async-start | bytes 4194304 | tf_op jit(solution)/shard_map/psum | solution.py:158
  8.3 14.8 %collective-permute-start = (f32[2,128,256]{2,1,0:T(8,128)S(1)}, f32[2,128,256]{2,1,0:T(8,128)S(1)}, u32[]{:S(2)}, u32[]{:S(2)}) collective-permute-start(f32[2,128,256]{2,1,0:T(8,128)S(1)} %get-tuple-element.1189), channel_id=1, source_target_pairs={{0,16},{16,32},{32,48},{48,64},{64,80},{80,96},{96,112},{1,17},{17... | collective-permute-start | bytes 786440 | tf_op jit(solution)/shard_map/ppermute | solution.py:36
  12.7 11.5 collective-permute-start.1
  25.3 18.8 %collective-permute-start.2 = (f32[2,512,128]{2,1,0:T(8,128)}, f32[2,512,128]{2,1,0:T(8,128)}, u32[]{:S(2)}, u32[]{:S(2)}) collective-permute-start(f32[2,512,128]{2,1,0:T(8,128)} %get-tuple-element.1180), channel_id=1, source_target_pairs={{0,1},{1,2},{2,3},{3,4},{4,5},{5,6},{6,7},{7,8},{8,9},{9,10},{10,1... | collective-permute-start | bytes 1572872 | tf_op jit(solution)/shard_map/ppermute | solution.py:36
  32.0 12.3 collective-permute-start.3
  85.9 47.9 %collective-permute-start.4 = (f32[2,128,512]{2,1,0:T(8,128)}, f32[2,128,512]{2,1,0:T(8,128)}, u32[]{:S(2)}, u32[]{:S(2)}) collective-permute-start(f32[2,128,512]{2,1,0:T(8,128)} %get-tuple-element.1165), channel_id=1, source_target_pairs={{0,16},{16,32},{32,48},{48,64},{64,80},{80,96},{96,112},{1,17},{17... | collective-permute-start | bytes 1572872 | tf_op jit(solution)/shard_map/ppermute | solution.py:26
  122.5 12.4 collective-permute-start.5
  125.4 539.8 %all-reduce.7.cloned.1.call-start = ((), (), s32[]{:S(2)}) async-start(), calls=%async_computation.1 | async-start | bytes 4194304 | tf_op jit(solution)/shard_map/psum | solution.py:158
  136.9 118.3 %collective-permute-start.6 = (f32[2,256,128]{2,1,0:T(8,128)}, f32[2,256,128]{2,1,0:T(8,128)}, u32[]{:S(2)}, u32[]{:S(2)}) collective-permute-start(f32[2,256,128]{2,1,0:T(8,128)} %get-tuple-element.1179), channel_id=1, source_target_pairs={{0,1},{1,2},{2,3},{3,4},{4,5},{5,6},{6,7},{7,8},{8,9},{9,10},{10,1... | collective-permute-start | bytes 786440 | tf_op jit(solution)/shard_map/ppermute | solution.py:26
  176.5 80.5 %collective-permute-start.7 = (f32[2,256,128]{2,1,0:T(8,128)}, f32[2,256,128]{2,1,0:T(8,128)S(1)}, u32[]{:S(2)}, u32[]{:S(2)}) collective-permute-start(f32[2,256,128]{2,1,0:T(8,128)} %get-tuple-element.1178), channel_id=1, source_target_pairs={{1,0},{2,1},{3,2},{4,3},{5,4},{6,5},{7,6},{8,7},{9,8},{10,9},{11,1... | collective-permute-start | bytes 786440 | tf_op jit(solution)/shard_map/ppermute | solution.py:26
  324.8 8.1 collective-permute-start.9
  334.0 20.9 %collective-permute-start.10 = (f32[2,512,128]{2,1,0:T(8,128)}, f32[2,512,128]{2,1,0:T(8,128)}, u32[]{:S(2)}, u32[]{:S(2)}) collective-permute-start(f32[2,512,128]{2,1,0:T(8,128)} %get-tuple-element.1176), channel_id=1, source_target_pairs={{0,1},{1,2},{2,3},{3,4},{4,5},{5,6},{6,7},{7,8},{8,9},{9,10},{10,1... | collective-permute-start | bytes 1572872 | tf_op jit(solution)/shard_map/ppermute | solution.py:36
  342.9 12.3 collective-permute-start.11
  428.2 12.2 collective-permute-start.12
  429.6 11.0 collective-permute-start.13
  441.6 15.2 %collective-permute-start.14 = (f32[2,256,128]{2,1,0:T(8,128)}, f32[2,256,128]{2,1,0:T(8,128)}, u32[]{:S(2)}, u32[]{:S(2)}) collective-permute-start(f32[2,256,128]{2,1,0:T(8,128)} %get-tuple-element.1175), channel_id=1, source_target_pairs={{0,1},{1,2},{2,3},{3,4},{4,5},{5,6},{6,7},{7,8},{8,9},{9,10},{10,1... | collective-permute-start | bytes 786440 | tf_op jit(solution)/shard_map/ppermute | solution.py:26
  451.8 31.5 %collective-permute-start.15 = (f32[2,256,128]{2,1,0:T(8,128)}, f32[2,256,128]{2,1,0:T(8,128)}, u32[]{:S(2)}, u32[]{:S(2)}) collective-permute-start(f32[2,256,128]{2,1,0:T(8,128)} %get-tuple-element.1174), channel_id=1, source_target_pairs={{1,0},{2,1},{3,2},{4,3},{5,4},{6,5},{7,6},{8,7},{9,8},{10,9},{11,1... | collective-permute-start | bytes 786440 | tf_op jit(solution)/shard_map/ppermute | solution.py:26
  456.7 515.8 %all-reduce.9.cloned.1.call-start = ((), (), s32[]{:S(2)}) async-start(), calls=%async_computation.2 | async-start | bytes 4194304 | tf_op jit(solution)/shard_map/psum | solution.py:158
  485.8 11.8 collective-permute-start.17
  498.7 170.4 %collective-permute-start.18 = (f32[2,512,128]{2,1,0:T(8,128)}, f32[2,512,128]{2,1,0:T(8,128)}, u32[]{:S(2)}, u32[]{:S(2)}) collective-permute-start(f32[2,512,128]{2,1,0:T(8,128)} %get-tuple-element.1172), channel_id=1, source_target_pairs={{0,1},{1,2},{2,3},{3,4},{4,5},{5,6},{6,7},{7,8},{8,9},{9,10},{10,1... | collective-permute-start | bytes 1572872 | tf_op jit(solution)/shard_map/ppermute | solution.py:36
  510.0 159.2 %collective-permute-start.19 = (f32[2,512,128]{2,1,0:T(8,128)}, f32[2,512,128]{2,1,0:T(8,128)}, u32[]{:S(2)}, u32[]{:S(2)}) collective-permute-start(f32[2,512,128]{2,1,0:T(8,128)} %get-tuple-element.1173), channel_id=1, source_target_pairs={{1,0},{2,1},{3,2},{4,3},{5,4},{6,5},{7,6},{8,7},{9,8},{10,9},{11,1... | collective-permute-start | bytes 1572872 | tf_op jit(solution)/shard_map/ppermute | solution.py:37
  709.1 49.2 %collective-permute-start.20 = (f32[2,128,512]{2,1,0:T(8,128)S(1)}, f32[2,128,512]{2,1,0:T(8,128)S(1)}, u32[]{:S(2)}, u32[]{:S(2)}) collective-permute-start(f32[2,128,512]{2,1,0:T(8,128)S(1)} %get-tuple-element.1160), channel_id=1, source_target_pairs={{0,16},{16,32},{32,48},{48,64},{64,80},{80,96},{96,112},{1,17},{17... | collective-permute-start | bytes 1572872 | tf_op jit(solution)/shard_map/ppermute | solution.py:26
  742.9 15.4 %collective-permute-start.21 = (f32[2,128,512]{2,1,0:T(8,128)S(1)}, f32[2,128,512]{2,1,0:T(8,128)S(1)}, u32[]{:S(2)}, u32[]{:S(2)}) collective-permute-start(f32[2,128,512]{2,1,0:T(8,128)S(1)} %get-tuple-element.1159), channel_id=1, source_target_pairs={{16,0},{32,16},{48,32},{64,48},{80,64},{96,80},{112,96},{17,1},{33... | collective-permute-start | bytes 1572872 | tf_op jit(solution)/shard_map/ppermute | solution.py:26
  759.4 38.5 %collective-permute-start.22 = (f32[2,256,128]{2,1,0:T(8,128)}, f32[2,256,128]{2,1,0:T(8,128)}, u32[]{:S(2)}, u32[]{:S(2)}) collective-permute-start(f32[2,256,128]{2,1,0:T(8,128)} %get-tuple-element.1171), channel_id=1, source_target_pairs={{0,1},{1,2},{2,3},{3,4},{4,5},{5,6},{6,7},{7,8},{8,9},{9,10},{10,1... | collective-permute-start | bytes 786440 | tf_op jit(solution)/shard_map/ppermute | solution.py:26
  792.9 9.5 collective-permute-start.23
  797.7 448.2 %all-reduce.11.cloned.1.call-start = ((), (), s32[]{:S(2)}) async-start(), calls=%async_computation.3 | async-start | bytes 4194304 | tf_op jit(solution)/shard_map/psum | solution.py:158
  807.1 9.4 collective-permute-start.25
  817.6 158.9 %collective-permute-start.26 = (f32[2,512,128]{2,1,0:T(8,128)}, f32[2,512,128]{2,1,0:T(8,128)}, u32[]{:S(2)}, u32[]{:S(2)}) collective-permute-start(f32[2,512,128]{2,1,0:T(8,128)} %get-tuple-element.1168), channel_id=1, source_target_pairs={{0,1},{1,2},{2,3},{3,4},{4,5},{5,6},{6,7},{7,8},{8,9},{9,10},{10,1... | collective-permute-start | bytes 1572872 | tf_op jit(solution)/shard_map/ppermute | solution.py:36
  822.4 154.2 %collective-permute-start.27 = (f32[2,512,128]{2,1,0:T(8,128)}, f32[2,512,128]{2,1,0:T(8,128)}, u32[]{:S(2)}, u32[]{:S(2)}) collective-permute-start(f32[2,512,128]{2,1,0:T(8,128)} %get-tuple-element.1169), channel_id=1, source_target_pairs={{1,0},{2,1},{3,2},{4,3},{5,4},{6,5},{7,6},{8,7},{9,8},{10,9},{11,1... | collective-permute-start | bytes 1572872 | tf_op jit(solution)/shard_map/ppermute | solution.py:37
  1051.7 13.4 %collective-permute-start.29 = (f32[2,128,512]{2,1,0:T(8,128)}, f32[2,128,512]{2,1,0:T(8,128)S(1)}, u32[]{:S(2)}, u32[]{:S(2)}) collective-permute-start(f32[2,128,512]{2,1,0:T(8,128)} %get-tuple-element.1157), channel_id=1, source_target_pairs={{16,0},{32,16},{48,32},{64,48},{80,64},{96,80},{112,96},{17,1},{33... | collective-permute-start | bytes 1572872 | tf_op jit(solution)/shard_map/ppermute | solution.py:26
  1069.0 153.1 %collective-permute-start.30 = (f32[2,256,128]{2,1,0:T(8,128)}, f32[2,256,128]{2,1,0:T(8,128)S(1)}, u32[]{:S(2)}, u32[]{:S(2)}) collective-permute-start(f32[2,256,128]{2,1,0:T(8,128)} %get-tuple-element.1167), channel_id=1, source_target_pairs={{0,1},{1,2},{2,3},{3,4},{4,5},{5,6},{6,7},{7,8},{8,9},{9,10},{10,1... | collective-permute-start | bytes 786440 | tf_op jit(solution)/shard_map/ppermute | solution.py:26
  1074.7 148.4 %collective-permute-start.31 = (f32[2,256,128]{2,1,0:T(8,128)}, f32[2,256,128]{2,1,0:T(8,128)S(1)}, u32[]{:S(2)}, u32[]{:S(2)}) collective-permute-start(f32[2,256,128]{2,1,0:T(8,128)} %get-tuple-element.1166), channel_id=1, source_target_pairs={{1,0},{2,1},{3,2},{4,3},{5,4},{6,5},{7,6},{8,7},{9,8},{10,9},{11,1... | collective-permute-start | bytes 786440 | tf_op jit(solution)/shard_map/ppermute | solution.py:26
  (43 other events, 1610.1 us)
Sparse Core Ops, SparseCore 0:
  125.5 190.6 all-reduce.4
  456.8 208.2 all-reduce.6
  797.9 174.6 all-reduce.8
  1055.7 190.1 all-reduce.10
where the time goes:
time: 1270 us; the launch traced here: 1260 us
  blocking collectives  392 us (31%)
  waiting for transfers between devices  321 us (25%)
  starting transfers between devices  231 us (18%)
  local copies, waits for them, and re-layouts  110 us (9%)
  other arithmetic  94.6 us (7%)
  matrix products  51.3 us (4%)
  loops' own time  35.8 us (3%)
  between operations  20.5 us (2%)
    psum x4, blocking collectives, on_device(): summed, power_total = lax.psum((probe_grad, power_sum), ROW_COL)  321 us
    psum x4, waiting for transfers between devices, on_device(): summed, power_total = lax.psum((probe_grad, power_sum), ROW_COL)  205 us
    ppermute x16, starting transfers between devices, shifted(): lax.ppermute(value, axis, [(source, source + steps) for source in range(l...  175 us
    psum x5, blocking collectives, over_axes(): return functools.reduce(lax.psum, axes, array)  71 us
    ppermute x16, waiting for transfers between devices, shifted(): lax.ppermute(value, axis, [(source, source + steps) for source in range(l...  69.4 us
    dot_general x12, matrix products, transform(): jnp.einsum('imxb,oiby->omxy', left_half, table, preferred_element_type=jn...  51.3 us
    ppermute x8, starting transfers between devices, padded(): before = lax.ppermute(last, axis, up)  42.8 us
    dynamic_update_slice x6, local copies, waits for them, and re-layouts, visit(): lax.dynamic_update_slice(object_grad, region + object_term, anchor)  39.3 us
  transfers between devices with their start and end apart: 36, of which 22 were waited for; matrix products, arithmetic and copies ran while one was open for 4% of the time, Pallas kernels for 0%

commit v1 on v0

v1 whole, which is shorter than its diff:
```python
import functools
import math

import jax
import jax.numpy as jnp
import numpy as np
from jax import lax
from jax.experimental import pallas as pl
from jax.experimental.pallas import tpu as pltpu
from jax.sharding import Mesh
from jax.sharding import PartitionSpec as P

BATCHES = 2
ITERS = 2
SLOTS = 3
MODES = 4
SIDE = 256
HALF = 128
EXT = 512
AXES = ("row_0", "row_1", "col_0", "col_1", "col_2")
ROW = ("row_0", "row_1")
COL = ("col_0", "col_1", "col_2")
F32 = jnp.float32
BF16 = jnp.bfloat16

object_rate = 0.9
probe_rate = 0.5
floor_value = 0.5
tiny_value = 1e-06


def transform_tables():
    index = np.arange(SIDE)
    angles = (index[:, None] * index[None, :] % SIDE) * (2.0 * math.pi / SIDE)
    scale = 1.0 / math.sqrt(SIDE)
    c = np.cos(angles) * scale
    s = -np.sin(angles) * scale
    left = np.block([[c, -s], [s, c]])
    return left.astype(jnp.bfloat16), left.T.astype(jnp.bfloat16)


def compute_body(
    batch, rows_ref, cols_ref, counts_ref, obj, probe, mags, left_tab, right_tab,
    grad, pgrad, stats, win, wave, half, field,
):
    CH = 16
    steps = SIDE // CH
    lane = lax.broadcasted_iota(jnp.int32, (CH, 128), 1)

    grad[...] = jnp.zeros_like(grad)
    pgrad[...] = jnp.zeros_like(pgrad)
    stats[...] = jnp.zeros_like(stats)

    def fold(x):
        total = x[0:8, :]
        for i in range(1, x.shape[0] // 8):
            total = total + x[8 * i:8 * i + 8, :]
        return total

    def visit(slot, carry):
        row0 = rows_ref[batch * SLOTS + slot]
        col0 = cols_ref[batch * SLOTS + slot]
        block = lax.shift_right_logical(col0, 7)
        shift = col0 & 127
        back = (128 - shift) & 127

        def make_exit(i, c):
            at = pl.multiple_of(i * CH, CH)
            w = []
            for p in range(2):
                rolled = [
                    pltpu.roll(obj[p, block + j, pl.ds(row0 + at, CH), :], back, 1) for j in range(3)
                ]
                keep = lane < 128 - shift
                w.append([jnp.where(keep, rolled[j], rolled[j + 1]) for j in range(2)])
            power = jnp.zeros((8, 128), F32)
            for j in range(2):
                wr, wi = w[0][j], w[1][j]
                win[0, j, pl.ds(at, CH), :] = wr
                win[1, j, pl.ds(at, CH), :] = wi
                power = power + fold(wr * wr + wi * wi)
                for k in range(MODES):
                    pr = probe[0, k, pl.ds(j * SIDE + at, CH), :]
                    pi = probe[1, k, pl.ds(j * SIDE + at, CH), :]
                    wave[k, pl.ds(at, CH), j * 128:(j + 1) * 128] = (pr * wr - pi * wi).astype(BF16)
                    wave[k, pl.ds(SIDE + at, CH), j * 128:(j + 1) * 128] = (pr * wi + pi * wr).astype(BF16)
            stats[0] = stats[0] + power
            return c

        lax.fori_loop(0, steps, make_exit, 0)

        def transform(first, second):
            def left(k, c):
                res = jnp.dot(first[...], wave[k], preferred_element_type=F32).astype(BF16)
                at = pl.multiple_of(k * SIDE, SIDE)
                half[pl.ds(at, SIDE), 0:SIDE] = res[0:SIDE]
                half[pl.ds(at, SIDE), SIDE:EXT] = res[SIDE:EXT]
                return c

            lax.fori_loop(0, MODES, left, 0)

            def right(k, c):
                at = pl.multiple_of(k * 512, 512)
                field[pl.ds(at, 512), :] = jnp.dot(
                    half[pl.ds(at, 512), :], second[...], preferred_element_type=F32
                )
                return c

            lax.fori_loop(0, 2, right, 0)

        transform(left_tab, right_tab)

        def correct(i, c):
            at = pl.multiple_of(i * CH, CH)
            parts = [
                (field[pl.ds(k * SIDE + at, CH), 0:SIDE], field[pl.ds(k * SIDE + at, CH), SIDE:EXT])
                for k in range(MODES)
            ]
            total = sum(re * re + im * im for re, im in parts)
            modulus = jnp.sqrt(total)
            amplitude = mags[0, 0, 0, slot, pl.ds(at, CH), :]
            factor = amplitude / jnp.maximum(modulus, floor_value) - 1.0
            gap = modulus - amplitude
            gap = gap * gap
            stats[1] = stats[1] + fold(gap[:, 0:128]) + fold(gap[:, 128:256])
            for k in range(MODES):
                wave[k, pl.ds(at, CH), :] = (parts[k][0] * factor).astype(BF16)
                wave[k, pl.ds(SIDE + at, CH), :] = (parts[k][1] * factor).astype(BF16)
            return c

        lax.fori_loop(0, steps, correct, 0)
        transform(right_tab, left_tab)

        def spread(i, c):
            at = pl.multiple_of(i * CH, CH)
            term = [[None, None], [None, None]]
            for j in range(2):
                wr = win[0, j, pl.ds(at, CH), :]
                wi = win[1, j, pl.ds(at, CH), :]
                tr = ti = None
                for k in range(MODES):
                    ur = field[pl.ds(k * SIDE + at, CH), j * 128:(j + 1) * 128]
                    ui = field[pl.ds(k * SIDE + at, CH), SIDE + j * 128:SIDE + (j + 1) * 128]
                    spot = pl.ds(j * SIDE + at, CH)
                    pr = probe[0, k, spot, :]
                    pi = probe[1, k, spot, :]
                    ar = pr * ur + pi * ui
                    ai = pr * ui - pi * ur
                    tr = ar if tr is None else tr + ar
                    ti = ai if ti is None else ti + ai
                    pgrad[0, k, spot, :] = pgrad[0, k, spot, :] + (wr * ur + wi * ui)
                    pgrad[1, k, spot, :] = pgrad[1, k, spot, :] + (wr * ui - wi * ur)
                term[0][j], term[1][j] = tr, ti
            low = lane < shift
            zero = jnp.zeros((CH, 128), F32)
            for p in range(2):
                a = pltpu.roll(term[p][0], shift, 1)
                b = pltpu.roll(term[p][1], shift, 1)
                adds = (jnp.where(low, zero, a), jnp.where(low, a, b), jnp.where(low, b, zero))
                for j in range(3):
                    spot = pl.ds(row0 + at, CH)
                    grad[p, block + j, spot, :] = grad[p, block + j, spot, :] + adds[j]
            return c

        lax.fori_loop(0, steps, spread, 0)
        return carry

    lax.fori_loop(0, counts_ref[batch], visit, 0)


def position_work(batch, pos_rows, pos_cols, counts, obj, probe, magnitudes, tables):
    whole = pl.BlockSpec(memory_space=pltpu.VMEM)
    smem = pl.BlockSpec(memory_space=pltpu.SMEM)
    mags = pl.BlockSpec((1, 1, 1, SLOTS, SIDE, SIDE), lambda i: (0, 0, batch, 0, 0, 0))
    flops = SLOTS * 2 * 2 * MODES * 4 * 2 * SIDE ** 3
    return pl.pallas_call(
        functools.partial(compute_body, batch),
        grid=(1,),
        out_shape=(
            jax.ShapeDtypeStruct((2, 4, EXT, 128), F32),
            jax.ShapeDtypeStruct((2, MODES, EXT, 128), F32),
            jax.ShapeDtypeStruct((2, 8, 128), F32),
        ),
        in_specs=[smem, smem, smem, whole, whole, mags, whole, whole],
        out_specs=(whole, whole, whole),
        scratch_shapes=[
            pltpu.VMEM((2, 2, SIDE, 128), F32),
            pltpu.VMEM((MODES, EXT, SIDE), BF16),
            pltpu.VMEM((MODES * SIDE, EXT), BF16),
            pltpu.VMEM((MODES * SIDE, EXT), F32),
        ],
        cost_estimate=pl.CostEstimate(flops=flops, bytes_accessed=12 << 20, transcendentals=0),
        compiler_params=pltpu.CompilerParams(vmem_limit_bytes=56 << 20),
        name="position_work",
    )(pos_rows, pos_cols, counts, obj, probe, magnitudes, *tables)


def where_am_i():
    y, lo, x, hi, core = (lax.axis_index(name) for name in AXES)
    row, col = y * 2 + lo, x * 4 + hi * 2 + core
    z = hi * 2 + lo

    def tile(r, c):
        return (r // 2, r % 2, c // 4, (c // 2) % 2, c % 2)

    def along(axis, value):
        if axis == "x":
            return (y, lo, value, hi, core)
        if axis == "y":
            return (value, lo, x, hi, core)
        return (y, value % 2, x, value // 2, core)

    partner = (y, lo, x, hi, 1 - core)
    coords = {"x": x, "y": y, "z": z}
    return row, col, core, coords, along, partner, tile


ORDERS = (("x", "y", "z"), ("y", "x", "z"))


def exchange_body(
    last, obj, probe, grad, pgrad, stats, obj_out, probe_out, stats_out,
    core_in, acc, one_in, one, two_in, two, three_in, tile_in, tile_sum, stat_core,
    col_in, row_in, mid, rdma_send, rdma_recv,
):
    row, col, core, coords, along, partner, tile = where_am_i()
    up, down = tile((row + 7) % 8, col), tile((row + 1) % 8, col)
    left, right = tile(row, (col + 15) % 16), tile(row, (col + 1) % 16)

    barrier = pltpu.get_barrier_semaphore()
    greeted = [partner, up, down, left, right]
    for axis in ("x", "y", "z"):
        for d in (1, 2, 3):
            greeted.append(along(axis, (coords[axis] + d) % 4))
    for peer in greeted:
        pl.semaphore_signal(barrier, inc=1, device_id=peer, device_id_type=pl.DeviceIdType.MESH)
    pl.semaphore_wait(barrier, len(greeted))

    count = [0]

    def send(src, dst, peer):
        n = count[0]
        count[0] += 1
        copy = pltpu.make_async_remote_copy(
            src_ref=src, dst_ref=dst, send_sem=rdma_send.at[n], recv_sem=rdma_recv.at[n],
            device_id=peer, device_id_type=pl.DeviceIdType.MESH,
        )
        copy.start()
        return copy

    def wait(copies):
        for copy in copies:
            copy.wait()

    cols_sent = [
        send(grad.at[:, 3], col_in.at[0], right),
        send(grad.at[:, 0], col_in.at[1], left),
    ]
    core_sent = [
        send(stats, stat_core, partner),
        send(pgrad.at[1 - core], core_in, partner),
    ]

    def peak_step(i, best):
        at = pl.multiple_of(i * 16, 16)
        total = None
        for p in range(2):
            for k in range(MODES):
                v = probe[p, k, pl.ds(at, 16), :]
                total = v * v if total is None else total + v * v
        return jnp.maximum(best, jnp.maximum(total[0:8], total[8:16]))

    best = lax.fori_loop(0, EXT // 16, peak_step, jnp.zeros((8, 128), F32))
    rate = object_rate / (jnp.max(best) + tiny_value)

    wait(core_sent)
    for k in range(MODES):
        acc[k] = pgrad[core, k] + core_in[k]
    tile_sum[...] = stats[...] + stat_core[...]

    def scatter(phase, source, landing, length):
        sent = []
        for d in (2, 1, 3):
            peer = along(ORDERS[0][phase], (coords[ORDERS[0][phase]] + d) % 4)
            sent.append(send(tile_sum, tile_in.at[phase, d - 1], peer))
            for g in range(2):
                axis = ORDERS[g][phase]
                to = (coords[axis] + d) % 4
                at = pl.multiple_of(to * length, length)
                sent.append(
                    send(
                        source.at[2 * g:2 * g + 2, pl.ds(at, length), :],
                        landing.at[d - 1, 2 * g:2 * g + 2],
                        along(axis, to),
                    )
                )
        return sent

    def gather_sum(phase, source, landing, length):
        out = []
        for g in range(2):
            at = pl.multiple_of(coords[ORDERS[g][phase]] * length, length)
            for k in (2 * g, 2 * g + 1):
                out.append(
                    source[k, pl.ds(at, length), :] + landing[0, k] + landing[1, k] + landing[2, k]
                )
        tile_sum[...] = tile_sum[...] + tile_in[phase, 0] + tile_in[phase, 1] + tile_in[phase, 2]
        return out

    sent = scatter(0, acc, one_in, 128)
    wait(sent)
    for k, v in enumerate(gather_sum(0, acc, one_in, 128)):
        one[k] = v
    sent = scatter(1, one, two_in, 32)

    wait(cols_sent)
    has_left, has_right = col > 0, col < 15
    for p in range(2):
        mid[p, 0] = grad[p, 1] + jnp.where(has_left, col_in[0, p], 0.0)
        mid[p, 1] = grad[p, 2] + jnp.where(has_right, col_in[1, p], 0.0)
    rows_sent = [
        send(mid.at[:, :, 0:SIDE, :], row_in.at[1], up),
        send(mid.at[:, :, SIDE:EXT, :], row_in.at[0], down),
    ]

    wait(sent)
    for k, v in enumerate(gather_sum(1, one, two_in, 32)):
        two[k] = v
    sent = scatter(2, two, three_in, 8)
    wait(sent)
    sums = gather_sum(2, two, three_in, 8)

    stats_out[...] = tile_sum[...]
    gain = probe_rate * SIDE * SIDE / jnp.sum(tile_sum[0])
    starts = []
    for g in range(2):
        a, b, c = (coords[axis] for axis in ORDERS[g])
        starts.append((a * 128, a * 128 + b * 32, a * 128 + b * 32 + c * 8))
    for k in range(MODES):
        at = pl.multiple_of(starts[k // 2][2], 8)
        probe_out[core, k, pl.ds(at, 8), :] = probe[core, k, pl.ds(at, 8), :] + gain * sums[k]

    def spread(phase, length):
        out = []
        for d in (2, 1, 3):
            for g in range(2):
                axis = ORDERS[g][phase]
                at = pl.multiple_of(starts[g][phase], length)
                block = probe_out.at[core, 2 * g:2 * g + 2, pl.ds(at, length), :]
                out.append(send(block, block, along(axis, (coords[axis] + d) % 4)))
        return out

    wait(spread(2, 8))
    out2 = spread(1, 32)

    def finish_rows():
        wait(rows_sent)
        has_up, has_down = row > 0, row < 7
        for p in range(2):
            for j in range(2):
                upper = jnp.where(has_up, row_in[0, p, j], 0.0)
                lower = jnp.where(has_down, row_in[1, p, j], 0.0)
                top = mid[p, j, 0:SIDE, :] + upper
                low = mid[p, j, SIDE:EXT, :] + lower
                old = obj[p, 1 + j]
                obj_out[p, 1 + j, 0:HALF, :] = old[0:HALF] + jnp.where(has_up, rate, 0.0) * top[0:HALF]
                obj_out[p, 1 + j, HALF:SIDE, :] = old[HALF:SIDE] + rate * top[HALF:SIDE]
                obj_out[p, 1 + j, SIDE:SIDE + HALF, :] = old[SIDE:SIDE + HALF] + rate * low[0:HALF]
                obj_out[p, 1 + j, SIDE + HALF:EXT, :] = (
                    old[SIDE + HALF:EXT] + jnp.where(has_down, rate, 0.0) * low[HALF:SIDE]
                )

    wait(out2)
    out1 = spread(0, 128)
    finish_rows()
    halo = []
    if not last:
        halo = [
            send(obj_out.at[:, 2], col_in.at[2], right),
            send(obj_out.at[:, 1], col_in.at[3], left),
        ]
    wait(out1)
    planes = probe_out.at[core]
    wait([send(planes, planes, partner)])
    if last:
        for p in range(2):
            obj_out[p, 0] = obj[p, 0]
            obj_out[p, 3] = obj[p, 3]
    else:
        wait(halo)
        for p in range(2):
            obj_out[p, 0] = jnp.where(has_left, col_in[2, p], 0.0)
            obj_out[p, 3] = jnp.where(has_right, col_in[3, p], 0.0)


def exchange(last, obj, probe, grad, pgrad, stats):
    whole = pl.BlockSpec(memory_space=pltpu.VMEM)
    messages = 64
    return pl.pallas_call(
        functools.partial(exchange_body, last),
        out_shape=(
            jax.ShapeDtypeStruct((2, 4, EXT, 128), F32),
            jax.ShapeDtypeStruct((2, MODES, EXT, 128), F32),
            jax.ShapeDtypeStruct((2, 8, 128), F32),
        ),
        in_specs=[whole] * 5,
        out_specs=(whole,) * 3,
        scratch_shapes=[
            pltpu.VMEM((MODES, EXT, 128), F32),
            pltpu.VMEM((MODES, EXT, 128), F32),
            pltpu.VMEM((3, MODES, 128, 128), F32),
            pltpu.VMEM((MODES, 128, 128), F32),
            pltpu.VMEM((3, MODES, 32, 128), F32),
            pltpu.VMEM((MODES, 32, 128), F32),
            pltpu.VMEM((3, MODES, 8, 128), F32),
            pltpu.VMEM((3, 3, 2, 8, 128), F32),
            pltpu.VMEM((2, 8, 128), F32),
            pltpu.VMEM((2, 8, 128), F32),
            pltpu.VMEM((4, 2, EXT, 128), F32),
            pltpu.VMEM((2, 2, 2, SIDE, 128), F32),
            pltpu.VMEM((2, 2, EXT, 128), F32),
            pltpu.SemaphoreType.DMA((messages,)),
            pltpu.SemaphoreType.DMA((messages,)),
        ],
        cost_estimate=pl.CostEstimate(flops=40 << 20, bytes_accessed=12 << 20, transcendentals=0),
        compiler_params=pltpu.CompilerParams(
            collective_id=1 if last else 0, has_side_effects=True, vmem_limit_bytes=48 << 20
        ),
        name="exchange_last" if last else "exchange",
    )(obj, probe, grad, pgrad, stats)


def padded(array, sides, width):
    for axis, dim in sides:
        devices, length = (lax.axis_size(axis), array.shape[dim])
        up = [(i, (i + 1) % devices) for i in range(devices - 1)]
        down = [(j, i) for i, j in up]
        last = lax.slice_in_dim(array, length - width, length, axis=dim)
        leading = lax.slice_in_dim(array, 0, width, axis=dim)
        before = lax.ppermute(last, axis, up)
        after = lax.ppermute(leading, axis, down)
        array = jnp.concatenate([before, array, after], axis=dim)
    return array


def on_device(object_field, probe, pos_rows, pos_cols, counts, magnitudes):
    tables = tuple(jnp.asarray(t) for t in transform_tables())
    rows, cols, live = pos_rows.reshape(-1), pos_cols.reshape(-1), counts.reshape(-1)
    extended = padded(object_field, ((ROW, 1), (COL, 2)), HALF)
    obj = extended.reshape(2, EXT, 4, 128).transpose(0, 2, 1, 3)
    planes = probe.reshape(2, MODES, SIDE, 2, 128).transpose(0, 1, 3, 2, 4)
    planes = planes.reshape(2, MODES, EXT, 128)
    misfits = []
    for update in range(ITERS * BATCHES):
        batch = update % BATCHES
        grad, pgrad, stats = position_work(batch, rows, cols, live, obj, planes, magnitudes, tables)
        last = update == ITERS * BATCHES - 1
        obj, planes, totals = exchange(last, obj, planes, grad, pgrad, stats)
        misfits.append(jnp.sum(totals[1]))
    out = obj[:, 1:3, HALF:HALF + SIDE, :].transpose(0, 2, 1, 3).reshape(2, SIDE, SIDE)
    probe_out = planes.reshape(2, MODES, 2, SIDE, 128).transpose(0, 1, 3, 2, 4)
    return (out, probe_out.reshape(2, MODES, SIDE, SIDE), jnp.stack(misfits))


def solution(mesh):
    finer = Mesh(mesh.devices.reshape(4, 2, 4, 2, 2), AXES)
    return jax.shard_map(
        on_device,
        mesh=finer,
        in_specs=(
            P(None, ROW, COL),
            P(),
            P(ROW, COL, None, None),
            P(ROW, COL, None, None),
            P(ROW, COL, None),
            P(ROW, COL, None, None, None, None),
        ),
        out_specs=(P(None, ROW, COL), P(), P()),
        check_vma=False,
    )
```

time: 1270 us -> 452 us (0.36); the launches traced: 1260 us -> 452 us
  blocking collectives: 392 us -> 0 us
  Pallas kernels: 0 us -> 387 us
  waiting for transfers between devices: 321 us -> 16.7 us
  starting transfers between devices: 231 us -> 14.3 us
  other arithmetic: 94.6 us -> 8.34 us
  local copies, waits for them, and re-layouts: 110 us -> 24.6 us
  matrix products: 51.3 us -> 0 us
  loops' own time: 35.8 us -> 0 us
  between operations: 20.5 us -> 0.81 us
    psum x9 -> x0, blocking collectives: 392 us -> none  [the longest x4 321 us: on_device(): summed, power_total = lax.psum((probe_grad, power_sum), ROW_COL)]
    pallas_call x0 -> x8, Pallas kernels: none -> 387 us  [the longest x4 301 us: exchange(): pl.pallas_call(functools.partial(exchange_body, last), out_shape=(jax.Sha...]
    psum x4 -> x0, waiting for transfers between devices: 205 us -> none  [on_device(): summed, power_total = lax.psum((probe_grad, power_sum), ROW_COL)]
    ppermute x16 -> x0, starting transfers between devices: 175 us -> none  [shifted(): lax.ppermute(value, axis, [(source, source + steps) for source in range(l...]
    ppermute x16 -> x0, waiting for transfers between devices: 69.4 us -> none  [shifted(): lax.ppermute(value, axis, [(source, source + steps) for source in range(l...]
    dot_general x12 -> x0, matrix products: 51.3 us -> none  [transform(): jnp.einsum('imxb,oiby->omxy', left_half, table, preferred_element_type=jn...]
    dynamic_update_slice x6 -> x0, local copies, waits for them, and re-layouts: 39.3 us -> none  [visit(): lax.dynamic_update_slice(object_grad, region + object_term, anchor)]
    add x23 -> x0, other arithmetic: 36.3 us -> none  [the longest x6 14.2 us: visit(): region + object_term]
  transfers between devices with their start and end apart: 36 -> 4, of which waited for: 22 -> 3; matrix products, arithmetic and copies ran while one was open for 4% -> 1% of each run, Pallas kernels for 0% -> 0%
where the time goes in v1:
time: 452 us
  Pallas kernels  387 us (86%)
  local copies, waits for them, and re-layouts  24.6 us (5%)
  waiting for transfers between devices  16.7 us (4%)
  starting transfers between devices  14.3 us (3%)
  other arithmetic  8.34 us (2%)
    pallas_call x4, Pallas kernels, exchange(): pl.pallas_call(functools.partial(exchange_body, last), out_shape=(jax.Sha...  301 us
    pallas_call x4, Pallas kernels, position_work(): pl.pallas_call(functools.partial(compute_body, batch), grid=(1,), out_sha...  85.6 us
    ppermute x2, waiting for transfers between devices, padded(): before = lax.ppermute(last, axis, up)  16.4 us
    unnamed x30, local copies, waits for them, and re-layouts  14.4 us
    ppermute x2, starting transfers between devices, padded(): before = lax.ppermute(last, axis, up)  11.1 us
  transfers between devices with their start and end apart: 4, of which 3 were waited for; matrix products, arithmetic and copies ran while one was open for 1% of the time, Pallas kernels for 0%

profile of v1, /device:TPU:1, one launch (start us, length us, event | category | flops | bytes accessed | tf_op | source)
XLA Modules:
  0.0 451.7 jit_solution(7665215700319243069)
XLA Ops:
  0.6 1.4 copy.13
  2.1 4.4 collective-permute-start
  6.5 1.3 collective-permute-start.1
  7.8 9.1 %collective-permute-done = f32[2,128,256]{1,2,0:T(8,128)S(1)} collective-permute-done((f32[2,128,256]{1,2,0:T(8,128)S(1)}, f32[2,128,256]{1,2,0:T(8,128)S(1)}, u32[]{:S(2)}, u32[]{:S(2)}) %collective-permute-start) | collective-permute-done | bytes 262176 | tf_op jit(solution)/shard_map/ppermute | solution.py:440
  17.0 1.0 fusion
  18.0 6.8 %collective-permute-start.2 = (f32[2,512,128]{1,2,0:T(8,128)}, f32[2,512,128]{1,2,0:T(8,128)}, u32[]{:S(2)}, u32[]{:S(2)}) collective-permute-start(f32[2,512,128]{1,2,0:T(8,128)} %get-tuple-element.54), channel_id=1, source_target_pairs={{0,1},{1,2},{2,3},{3,4},{4,5},{5,6},{6,7},{7,8},{8,9},{9,10},{10,1... | collective-permute-start | bytes 1572872 | tf_op jit(solution)/shard_map/ppermute | solution.py:440
  24.8 1.9 collective-permute-start.3
  28.0 1.6 copy_bitcast_fusion.1
  29.6 7.3 %collective-permute-done.2 = f32[2,512,128]{1,2,0:T(8,128)} collective-permute-done((f32[2,512,128]{1,2,0:T(8,128)}, f32[2,512,128]{1,2,0:T(8,128)}, u32[]{:S(2)}, u32[]{:S(2)}) %collective-permute-start.2) | collective-permute-done | bytes 524320 | tf_op jit(solution)/shard_map/ppermute | solution.py:440
  37.1 2.8 pad_maximum_fusion
  39.9 2.9 copy.16
  42.8 21.4 %position_work.4 = (f32[2,4,512,128]{3,2,1,0:T(8,128)}, f32[2,4,512,128]{3,2,1,0:T(8,128)}, f32[2,8,128]{2,1,0:T(8,128)}) custom-call(s32[6]{0:T(128)} %reshape.36.rows_ref, s32[6]{0:T(128)} %reshape.37.cols_ref, s32[2]{0:T(128)} %bitcast.33, f32[2,4,512,128]{3,2,1,0:T(8,128)} %bitcast.28, f32[2,4,512,128]{3,2,1,0:T(8,128)} %bitcast.26, ...), custom_call_target="tpu_custom_call" | custom-call | flops 6442450944 | bytes 12582912 | tf_op jit(solution)/shard_map/position_work/pallas_call | solution.py:176
  64.2 0.7 copy-done.9
  64.9 80.9 %exchange.3 = (f32[2,4,512,128]{3,2,1,0:T(8,128)S(1)}, f32[2,4,512,128]{3,2,1,0:T(8,128)S(1)}, f32[2,8,128]{2,1,0:T(8,128)S(1)}) custom-call(f32[2,4,512,128]{3,2,1,0:T(8,128)} %bitcast.29, f32[2,4,512,128]{3,2,1,0:T(8,128)} %bitcast.27, f32[2,4,512,128]{3,2,1,0:T(8,128)} %get-tuple-element.27.grad, f32[2,4,512,128]{3,2,1,0:T(8,128)} %get-tuple-element.28.pgrad, ...), custom_call_target="tpu_custom_call" | custom-call | flops 41943040 | bytes 12582912 | tf_op jit(solution)/shard_map/exchange/pallas_call | solution.py:399
  145.8 1.3 copy-done.3
  147.1 1.3 copy-done.4
  149.1 21.4 %position_work.5 = (f32[2,4,512,128]{3,2,1,0:T(8,128)}, f32[2,4,512,128]{3,2,1,0:T(8,128)}, f32[2,8,128]{2,1,0:T(8,128)}) custom-call(s32[6]{0:T(128)} %reshape.36.rows_ref, s32[6]{0:T(128)} %reshape.37.cols_ref, s32[2]{0:T(128)} %bitcast.34, f32[2,4,512,128]{3,2,1,0:T(8,128)} %copy-done.3, f32[2,4,512,128]{3,2,1,0:T(8,128)} %copy-done.4, ...), custom_call_target="tpu_custom_call" | custom-call | flops 6442450944 | bytes 12582912 | tf_op jit(solution)/shard_map/position_work/pallas_call | solution.py:176
  170.5 0.7 copy-done.10
  171.2 74.4 %exchange.4 = (f32[2,4,512,128]{3,2,1,0:T(8,128)S(1)}, f32[2,4,512,128]{3,2,1,0:T(8,128)S(1)}, f32[2,8,128]{2,1,0:T(8,128)S(1)}) custom-call(f32[2,4,512,128]{3,2,1,0:T(8,128)} %copy-done.3, f32[2,4,512,128]{3,2,1,0:T(8,128)} %copy-done.4, f32[2,4,512,128]{3,2,1,0:T(8,128)} %get-tuple-element.32.grad, f32[2,4,512,128]{3,2,1,0:T(8,128)} %get-tuple-element.33.pgrad, ...), custom_call_target="tpu_custom_call" | custom-call | flops 41943040 | bytes 12582912 | tf_op jit(solution)/shard_map/exchange/pallas_call | solution.py:399
  245.6 1.3 copy-done.5
  246.9 1.3 copy-done.6
  248.9 21.4 %position_work.6 = (f32[2,4,512,128]{3,2,1,0:T(8,128)}, f32[2,4,512,128]{3,2,1,0:T(8,128)}, f32[2,8,128]{2,1,0:T(8,128)}) custom-call(s32[6]{0:T(128)} %reshape.36.rows_ref, s32[6]{0:T(128)} %reshape.37.cols_ref, s32[2]{0:T(128)} %bitcast.35, f32[2,4,512,128]{3,2,1,0:T(8,128)} %copy-done.5, f32[2,4,512,128]{3,2,1,0:T(8,128)} %copy-done.6, ...), custom_call_target="tpu_custom_call" | custom-call | flops 6442450944 | bytes 12582912 | tf_op jit(solution)/shard_map/position_work/pallas_call | solution.py:176
  270.3 0.7 copy-done.11
  271.0 76.1 %exchange.5 = (f32[2,4,512,128]{3,2,1,0:T(8,128)S(1)}, f32[2,4,512,128]{3,2,1,0:T(8,128)S(1)}, f32[2,8,128]{2,1,0:T(8,128)S(1)}) custom-call(f32[2,4,512,128]{3,2,1,0:T(8,128)} %copy-done.5, f32[2,4,512,128]{3,2,1,0:T(8,128)} %copy-done.6, f32[2,4,512,128]{3,2,1,0:T(8,128)} %get-tuple-element.37.grad, f32[2,4,512,128]{3,2,1,0:T(8,128)} %get-tuple-element.38.pgrad, ...), custom_call_target="tpu_custom_call" | custom-call | flops 41943040 | bytes 12582912 | tf_op jit(solution)/shard_map/exchange/pallas_call | solution.py:399
  347.1 1.3 copy-done.1
  348.4 1.3 copy-done.2
  350.3 21.4 %position_work.7 = (f32[2,4,512,128]{3,2,1,0:T(8,128)}, f32[2,4,512,128]{3,2,1,0:T(8,128)}, f32[2,8,128]{2,1,0:T(8,128)}) custom-call(s32[6]{0:T(128)} %reshape.36.rows_ref, s32[6]{0:T(128)} %reshape.37.cols_ref, s32[2]{0:T(128)} %bitcast.36, f32[2,4,512,128]{3,2,1,0:T(8,128)} %copy-done.1, f32[2,4,512,128]{3,2,1,0:T(8,128)} %copy-done.2, ...), custom_call_target="tpu_custom_call" | custom-call | flops 6442450944 | bytes 12582912 | tf_op jit(solution)/shard_map/position_work/pallas_call | solution.py:176
  372.5 69.9 %exchange_last.1 = (f32[2,4,512,128]{3,2,1,0:T(8,128)S(1)}, f32[2,4,512,128]{3,2,1,0:T(8,128)S(1)}, f32[2,8,128]{2,1,0:T(8,128)S(1)}) custom-call(f32[2,4,512,128]{3,2,1,0:T(8,128)} %copy-done.1, f32[2,4,512,128]{3,2,1,0:T(8,128)} %copy-done.2, f32[2,4,512,128]{3,2,1,0:T(8,128)} %get-tuple-element.42.grad, f32[2,4,512,128]{3,2,1,0:T(8,128)} %get-tuple-element.43.pgrad, ...), custom_call_target="tpu_custom_call" | custom-call | flops 41943040 | bytes 12582912 | tf_op jit(solution)/shard_map/exchange_last/pallas_call | solution.py:399
  442.4 1.3 copy-done.7
  444.6 1.0 copy.20
  445.6 3.1 copy.25
  448.6 3.0 pad_maximum_fusion.2
  (30 shorter events, 5.1 us)
Async XLA Ops:
  0.6 27.4 %copy-start = (f32[2,4,256,256]{3,2,1,0:T(8,128)S(1)}, f32[2,4,256,256]{3,2,1,0:T(8,128)}, u32[]{:S(2)}) copy-start(f32[2,4,256,256]{3,2,1,0:T(8,128)} %param.9) | copy-start | bytes 6291460
  2.1 14.8 %collective-permute-start = (f32[2,128,256]{1,2,0:T(8,128)S(1)}, f32[2,128,256]{1,2,0:T(8,128)S(1)}, u32[]{:S(2)}, u32[]{:S(2)}) collective-permute-start(f32[2,128,256]{1,2,0:T(8,128)S(1)} %get-tuple-element.56), channel_id=1, source_target_pairs={{0,16},{16,32},{32,48},{48,64},{64,80},{80,96},{96,112},{1,17},{17... | collective-permute-start | bytes 786440 | tf_op jit(solution)/shard_map/ppermute | solution.py:440
  6.5 20.3 %copy-start.12 = (s32[1,1,2,3]{3,2,1,0:T(2,128)S(1)}, s32[1,1,2,3]{3,2,1,0:T(2,128)}, u32[]{:S(2)}) copy-start(s32[1,1,2,3]{3,2,1,0:T(2,128)} %param.10) | copy-start | bytes 76
  6.5 20.9 %copy-start.13 = (s32[1,1,2,3]{3,2,1,0:T(2,128)S(1)}, s32[1,1,2,3]{3,2,1,0:T(2,128)}, u32[]{:S(2)}) copy-start(s32[1,1,2,3]{3,2,1,0:T(2,128)} %param.11) | copy-start | bytes 76
  6.5 10.4 %collective-permute-start.1 = (f32[2,128,256]{1,2,0:T(8,128)S(1)}, f32[2,128,256]{1,2,0:T(8,128)S(1)}, u32[]{:S(2)}, u32[]{:S(2)}) collective-permute-start(f32[2,128,256]{1,2,0:T(8,128)S(1)} %get-tuple-element.57), channel_id=1, source_target_pairs={{16,0},{32,16},{48,32},{64,48},{80,64},{96,80},{112,96},{17,1},{33... | collective-permute-start | bytes 786440 | tf_op jit(solution)/shard_map/ppermute | solution.py:441
  18.0 18.8 %collective-permute-start.2 = (f32[2,512,128]{1,2,0:T(8,128)}, f32[2,512,128]{1,2,0:T(8,128)}, u32[]{:S(2)}, u32[]{:S(2)}) collective-permute-start(f32[2,512,128]{1,2,0:T(8,128)} %get-tuple-element.54), channel_id=1, source_target_pairs={{0,1},{1,2},{2,3},{3,4},{4,5},{5,6},{6,7},{7,8},{8,9},{9,10},{10,1... | collective-permute-start | bytes 1572872 | tf_op jit(solution)/shard_map/ppermute | solution.py:440
  24.8 12.3 %collective-permute-start.3 = (f32[2,512,128]{1,2,0:T(8,128)}, f32[2,512,128]{1,2,0:T(8,128)}, u32[]{:S(2)}, u32[]{:S(2)}) collective-permute-start(f32[2,512,128]{1,2,0:T(8,128)} %get-tuple-element.55), channel_id=1, source_target_pairs={{1,0},{2,1},{3,2},{4,3},{5,4},{6,5},{7,6},{8,7},{9,8},{10,9},{11,1... | collective-permute-start | bytes 1572872 | tf_op jit(solution)/shard_map/ppermute | solution.py:441
  64.2 0.7 copy-start.9
  145.8 1.3 copy-start.3
  147.1 1.3 copy-start.4
  170.5 0.7 copy-start.10
  245.6 1.3 copy-start.5
  246.9 1.3 copy-start.6
  270.3 0.7 copy-start.11
  347.1 1.3 copy-start.1
  348.4 1.3 copy-start.2
  371.8 0.7 copy-start.8
  442.4 1.3 copy-start.7

commit v2 on v1

--- a/solution.py
+++ b/solution.py
@@ -220,12 +220,13 @@
 
 def exchange_body(
     last, obj, probe, grad, pgrad, stats, obj_out, probe_out, stats_out,
-    core_in, acc, one_in, one, two_in, two, three_in, tile_in, tile_sum, stat_core,
+    core_in, acc, one_in, one, two_in, z_in, tile_in, tile_z, tile_core,
     col_in, row_in, mid, rdma_send, rdma_recv,
 ):
     row, col, core, coords, along, partner, tile = where_am_i()
     up, down = tile((row + 7) % 8, col), tile((row + 1) % 8, col)
     left, right = tile(row, (col + 15) % 16), tile(row, (col + 1) % 16)
+    has_left, has_right, has_up, has_down = col > 0, col < 15, row > 0, row < 7
 
     barrier = pltpu.get_barrier_semaphore()
     greeted = [partner, up, down, left, right]
@@ -252,13 +253,13 @@
         for copy in copies:
             copy.wait()
 
+    core_sent = [
+        send(stats, tile_core, partner),
+        send(pgrad.at[1 - core], core_in, partner),
+    ]
     cols_sent = [
-        send(grad.at[:, 3], col_in.at[0], right),
-        send(grad.at[:, 0], col_in.at[1], left),
-    ]
-    core_sent = [
-        send(stats, stat_core, partner),
-        send(pgrad.at[1 - core], core_in, partner),
+        [send(grad.at[p, 3], col_in.at[0, p], right), send(grad.at[p, 0], col_in.at[1, p], left)]
+        for p in range(2)
     ]
 
     def peak_step(i, best):
@@ -273,16 +274,13 @@
     best = lax.fori_loop(0, EXT // 16, peak_step, jnp.zeros((8, 128), F32))
     rate = object_rate / (jnp.max(best) + tiny_value)
 
-    wait(core_sent)
-    for k in range(MODES):
-        acc[k] = pgrad[core, k] + core_in[k]
-    tile_sum[...] = stats[...] + stat_core[...]
-
-    def scatter(phase, source, landing, length):
+    def scatter(phase, source, landing, length, tile_value):
+        me = coords[ORDERS[0][phase]]
+        tile_in[phase, me] = tile_value
+        slot = tile_in.at[phase, me]
         sent = []
         for d in (2, 1, 3):
-            peer = along(ORDERS[0][phase], (coords[ORDERS[0][phase]] + d) % 4)
-            sent.append(send(tile_sum, tile_in.at[phase, d - 1], peer))
+            sent.append(send(slot, slot, along(ORDERS[0][phase], (me + d) % 4)))
             for g in range(2):
                 axis = ORDERS[g][phase]
                 to = (coords[axis] + d) % 4
@@ -304,84 +302,122 @@
                 out.append(
                     source[k, pl.ds(at, length), :] + landing[0, k] + landing[1, k] + landing[2, k]
                 )
-        tile_sum[...] = tile_sum[...] + tile_in[phase, 0] + tile_in[phase, 1] + tile_in[phase, 2]
         return out
 
-    sent = scatter(0, acc, one_in, 128)
+    def tile_total(phase):
+        return (tile_in[phase, 0] + tile_in[phase, 1]) + (tile_in[phase, 2] + tile_in[phase, 3])
+
+    def send_rows(p, j):
+        return [
+            send(mid.at[p, j, 0:SIDE, :], row_in.at[1, p, j], up),
+            send(mid.at[p, j, SIDE:EXT, :], row_in.at[0, p, j], down),
+        ]
+
+    def make_mid(p):
+        wait(cols_sent[p])
+        mid[p, 0] = grad[p, 1] + jnp.where(has_left, col_in[0, p], 0.0)
+        mid[p, 1] = grad[p, 2] + jnp.where(has_right, col_in[1, p], 0.0)
+
+    def update_object(p, j):
+        upper = jnp.where(has_up, row_in[0, p, j], 0.0)
+        lower = jnp.where(has_down, row_in[1, p, j], 0.0)
+        top = mid[p, j, 0:SIDE, :] + upper
+        low = mid[p, j, SIDE:EXT, :] + lower
+        old = obj[p, 1 + j]
+        obj_out[p, 1 + j, 0:HALF, :] = old[0:HALF] + jnp.where(has_up, rate, 0.0) * top[0:HALF]
+        obj_out[p, 1 + j, HALF:SIDE, :] = old[HALF:SIDE] + rate * top[HALF:SIDE]
+        obj_out[p, 1 + j, SIDE:SIDE + HALF, :] = old[SIDE:SIDE + HALF] + rate * low[0:HALF]
+        obj_out[p, 1 + j, SIDE + HALF:EXT, :] = (
+            old[SIDE + HALF:EXT] + jnp.where(has_down, rate, 0.0) * low[HALF:SIDE]
+        )
+
+    def send_halo(p):
+        if last:
+            return []
+        return [
+            send(obj_out.at[p, 2], col_in.at[2, p], right),
+            send(obj_out.at[p, 1], col_in.at[3, p], left),
+        ]
+
+    wait(core_sent)
+    for k in range(MODES):
+        acc[k] = pgrad[core, k] + core_in[k]
+    sent = scatter(0, acc, one_in, 128, stats[...] + tile_core[...])
+
+    make_mid(0)
+    rows_sent = [send_rows(0, 0), send_rows(0, 1)]
+
     wait(sent)
     for k, v in enumerate(gather_sum(0, acc, one_in, 128)):
         one[k] = v
-    sent = scatter(1, one, two_in, 32)
-
-    wait(cols_sent)
-    has_left, has_right = col > 0, col < 15
-    for p in range(2):
-        mid[p, 0] = grad[p, 1] + jnp.where(has_left, col_in[0, p], 0.0)
-        mid[p, 1] = grad[p, 2] + jnp.where(has_right, col_in[1, p], 0.0)
-    rows_sent = [
-        send(mid.at[:, :, 0:SIDE, :], row_in.at[1], up),
-        send(mid.at[:, :, SIDE:EXT, :], row_in.at[0], down),
-    ]
+    sent = scatter(1, one, two_in, 32, tile_total(0))
+
+    make_mid(1)
 
     wait(sent)
+    z = coords["z"]
     for k, v in enumerate(gather_sum(1, one, two_in, 32)):
-        two[k] = v
-    sent = scatter(2, two, three_in, 8)
+        z_in[z, k] = v
+    tile_z[z] = tile_total(1)
+    sent = []
+    for d in (2, 1, 3):
+        peer = along("z", (z + d) % 4)
+        sent.append(send(tile_z.at[z], tile_z.at[z], peer))
+        sent.append(send(z_in.at[z], z_in.at[z], peer))
+    rows_sent.append(send_rows(1, 0))
     wait(sent)
-    sums = gather_sum(2, two, three_in, 8)
-
-    stats_out[...] = tile_sum[...]
-    gain = probe_rate * SIDE * SIDE / jnp.sum(tile_sum[0])
+
+    totals = (tile_z[0] + tile_z[1]) + (tile_z[2] + tile_z[3])
+    stats_out[...] = totals
+    gain = probe_rate * SIDE * SIDE / jnp.sum(totals[0])
     starts = []
     for g in range(2):
-        a, b, c = (coords[axis] for axis in ORDERS[g])
-        starts.append((a * 128, a * 128 + b * 32, a * 128 + b * 32 + c * 8))
+        a, b = coords[ORDERS[g][0]], coords[ORDERS[g][1]]
+        starts.append((a * 128, a * 128 + b * 32))
     for k in range(MODES):
-        at = pl.multiple_of(starts[k // 2][2], 8)
-        probe_out[core, k, pl.ds(at, 8), :] = probe[core, k, pl.ds(at, 8), :] + gain * sums[k]
+        spot = pl.ds(pl.multiple_of(starts[k // 2][1], 32), 32)
+        total = (z_in[0, k] + z_in[1, k]) + (z_in[2, k] + z_in[3, k])
+        probe_out[core, k, spot, :] = probe[core, k, spot, :] + gain * total
+
+    def block_of(g, at, length):
+        at = pl.multiple_of(at, length)
+        return probe_out.at[core, 2 * g:2 * g + 2, pl.ds(at, length), :]
 
     def spread(phase, length):
-        out = []
+        out = {}
         for d in (2, 1, 3):
             for g in range(2):
                 axis = ORDERS[g][phase]
-                at = pl.multiple_of(starts[g][phase], length)
-                block = probe_out.at[core, 2 * g:2 * g + 2, pl.ds(at, length), :]
-                out.append(send(block, block, along(axis, (coords[axis] + d) % 4)))
+                block = block_of(g, starts[g][phase], length)
+                out[d, g] = send(block, block, along(axis, (coords[axis] + d) % 4))
         return out
 
-    wait(spread(2, 8))
     out2 = spread(1, 32)
-
-    def finish_rows():
-        wait(rows_sent)
-        has_up, has_down = row > 0, row < 7
-        for p in range(2):
-            for j in range(2):
-                upper = jnp.where(has_up, row_in[0, p, j], 0.0)
-                lower = jnp.where(has_down, row_in[1, p, j], 0.0)
-                top = mid[p, j, 0:SIDE, :] + upper
-                low = mid[p, j, SIDE:EXT, :] + lower
-                old = obj[p, 1 + j]
-                obj_out[p, 1 + j, 0:HALF, :] = old[0:HALF] + jnp.where(has_up, rate, 0.0) * top[0:HALF]
-                obj_out[p, 1 + j, HALF:SIDE, :] = old[HALF:SIDE] + rate * top[HALF:SIDE]
-                obj_out[p, 1 + j, SIDE:SIDE + HALF, :] = old[SIDE:SIDE + HALF] + rate * low[0:HALF]
-                obj_out[p, 1 + j, SIDE + HALF:EXT, :] = (
-                    old[SIDE + HALF:EXT] + jnp.where(has_down, rate, 0.0) * low[HALF:SIDE]
-                )
-
-    wait(out2)
+    rows_sent.append(send_rows(1, 1))
+    wait(out2.values())
     out1 = spread(0, 128)
-    finish_rows()
-    halo = []
-    if not last:
-        halo = [
-            send(obj_out.at[:, 2], col_in.at[2], right),
-            send(obj_out.at[:, 1], col_in.at[3], left),
-        ]
-    wait(out1)
-    planes = probe_out.at[core]
-    wait([send(planes, planes, partner)])
+    to_core = []
+    for g in range(2):
+        block = block_of(g, starts[g][0], 128)
+        to_core.append(send(block, block, partner))
+
+    wait(rows_sent[0] + rows_sent[1])
+    for j in range(2):
+        update_object(0, j)
+    halo = send_halo(0)
+
+    for d in (1, 3, 2):
+        for g in range(2):
+            out1[d, g].wait()
+            axis = ORDERS[g][0]
+            block = block_of(g, (coords[axis] + 4 - d) % 4 * 128, 128)
+            to_core.append(send(block, block, partner))
+
+    wait(rows_sent[2] + rows_sent[3])
+    for j in range(2):
+        update_object(1, j)
+    halo += send_halo(1)
+    wait(to_core)
     if last:
         for p in range(2):
             obj_out[p, 0] = obj[p, 0]
@@ -395,7 +431,7 @@
 
 def exchange(last, obj, probe, grad, pgrad, stats):
     whole = pl.BlockSpec(memory_space=pltpu.VMEM)
-    messages = 64
+    messages = 72
     return pl.pallas_call(
         functools.partial(exchange_body, last),
         out_shape=(
@@ -411,10 +447,9 @@
             pltpu.VMEM((3, MODES, 128, 128), F32),
             pltpu.VMEM((MODES, 128, 128), F32),
             pltpu.VMEM((3, MODES, 32, 128), F32),
-            pltpu.VMEM((MODES, 32, 128), F32),
-            pltpu.VMEM((3, MODES, 8, 128), F32),
-            pltpu.VMEM((3, 3, 2, 8, 128), F32),
-            pltpu.VMEM((2, 8, 128), F32),
+            pltpu.VMEM((4, MODES, 32, 128), F32),
+            pltpu.VMEM((2, 4, 2, 8, 128), F32),
+            pltpu.VMEM((4, 2, 8, 128), F32),
             pltpu.VMEM((2, 8, 128), F32),
             pltpu.VMEM((4, 2, EXT, 128), F32),
             pltpu.VMEM((2, 2, 2, SIDE, 128), F32),

time: 452 us -> 417 us (0.923)
  Pallas kernels: 387 us -> 353 us
    pallas_call x4, Pallas kernels: 301 us -> 267 us  [exchange(): pl.pallas_call(functools.partial(exchange_body, last), out_shape=(jax.Sha...]
where the time goes in v2:
time: 417 us; the launch traced here: 418 us
  Pallas kernels  353 us (85%)
  local copies, waits for them, and re-layouts  24.6 us (6%)
  waiting for transfers between devices  16.7 us (4%)
  starting transfers between devices  14.3 us (3%)
  other arithmetic  8.34 us (2%)
    pallas_call x4, Pallas kernels, exchange(): pl.pallas_call(functools.partial(exchange_body, last), out_shape=(jax.Sha...  267 us
    pallas_call x4, Pallas kernels, position_work(): pl.pallas_call(functools.partial(compute_body, batch), grid=(1,), out_sha...  85.6 us
    ppermute x2, waiting for transfers between devices, padded(): before = lax.ppermute(last, axis, up)  16.4 us
    unnamed x30, local copies, waits for them, and re-layouts  14.4 us
    ppermute x2, starting transfers between devices, padded(): before = lax.ppermute(last, axis, up)  11.1 us
  transfers between devices with their start and end apart: 4, of which 3 were waited for; matrix products, arithmetic and copies ran while one was open for 1% of the time, Pallas kernels for 0%

profile of v2, /device:TPU:1, one launch (start us, length us, event | category | flops | bytes accessed | tf_op | source)
XLA Modules:
  0.0 417.7 jit_solution(6384368640110965767)
XLA Ops:
  0.6 1.4 copy.13
  2.1 4.4 %collective-permute-start = (f32[2,128,256]{1,2,0:T(8,128)S(1)}, f32[2,128,256]{1,2,0:T(8,128)S(1)}, u32[]{:S(2)}, u32[]{:S(2)}) collective-permute-start(f32[2,128,256]{1,2,0:T(8,128)S(1)} %get-tuple-element.56), channel_id=1, source_target_pairs={{0,16},{16,32},{32,48},{48,64},{64,80},{80,96},{96,112},{1,17},{17... | collective-permute-start | bytes 786440 | tf_op jit(solution)/shard_map/ppermute | solution.py:475
  6.5 1.3 collective-permute-start.1
  7.8 9.1 %collective-permute-done = f32[2,128,256]{1,2,0:T(8,128)S(1)} collective-permute-done((f32[2,128,256]{1,2,0:T(8,128)S(1)}, f32[2,128,256]{1,2,0:T(8,128)S(1)}, u32[]{:S(2)}, u32[]{:S(2)}) %collective-permute-start) | collective-permute-done | bytes 262176 | tf_op jit(solution)/shard_map/ppermute | solution.py:475
  17.0 1.0 fusion
  18.0 6.8 %collective-permute-start.2 = (f32[2,512,128]{1,2,0:T(8,128)}, f32[2,512,128]{1,2,0:T(8,128)}, u32[]{:S(2)}, u32[]{:S(2)}) collective-permute-start(f32[2,512,128]{1,2,0:T(8,128)} %get-tuple-element.54), channel_id=1, source_target_pairs={{0,1},{1,2},{2,3},{3,4},{4,5},{5,6},{6,7},{7,8},{8,9},{9,10},{10,1... | collective-permute-start | bytes 1572872 | tf_op jit(solution)/shard_map/ppermute | solution.py:475
  24.8 1.9 collective-permute-start.3
  28.0 1.6 copy_bitcast_fusion.1
  29.6 7.3 %collective-permute-done.2 = f32[2,512,128]{1,2,0:T(8,128)} collective-permute-done((f32[2,512,128]{1,2,0:T(8,128)}, f32[2,512,128]{1,2,0:T(8,128)}, u32[]{:S(2)}, u32[]{:S(2)}) %collective-permute-start.2) | collective-permute-done | bytes 524320 | tf_op jit(solution)/shard_map/ppermute | solution.py:475
  37.1 2.8 pad_maximum_fusion
  39.9 2.9 copy.16
  42.8 13.2 %position_work.4 = (f32[2,4,512,128]{3,2,1,0:T(8,128)}, f32[2,4,512,128]{3,2,1,0:T(8,128)}, f32[2,8,128]{2,1,0:T(8,128)}) custom-call(s32[6]{0:T(128)} %reshape.36.rows_ref, s32[6]{0:T(128)} %reshape.37.cols_ref, s32[2]{0:T(128)} %bitcast.33, f32[2,4,512,128]{3,2,1,0:T(8,128)} %bitcast.28, f32[2,4,512,128]{3,2,1,0:T(8,128)} %bitcast.26, ...), custom_call_target="tpu_custom_call" | custom-call | flops 6442450944 | bytes 12582912 | tf_op jit(solution)/shard_map/position_work/pallas_call | solution.py:176
  56.0 0.7 copy-done.9
  56.7 79.7 %exchange.3 = (f32[2,4,512,128]{3,2,1,0:T(8,128)S(1)}, f32[2,4,512,128]{3,2,1,0:T(8,128)S(1)}, f32[2,8,128]{2,1,0:T(8,128)S(1)}) custom-call(f32[2,4,512,128]{3,2,1,0:T(8,128)} %bitcast.29, f32[2,4,512,128]{3,2,1,0:T(8,128)} %bitcast.27, f32[2,4,512,128]{3,2,1,0:T(8,128)} %get-tuple-element.27.grad, f32[2,4,512,128]{3,2,1,0:T(8,128)} %get-tuple-element.28.pgrad, ...), custom_call_target="tpu_custom_call" | custom-call | flops 41943040 | bytes 12582912 | tf_op jit(solution)/shard_map/exchange/pallas_call | solution.py:435
  136.4 1.3 copy-done.3
  137.7 1.3 copy-done.4
  139.7 29.6 %position_work.5 = (f32[2,4,512,128]{3,2,1,0:T(8,128)}, f32[2,4,512,128]{3,2,1,0:T(8,128)}, f32[2,8,128]{2,1,0:T(8,128)}) custom-call(s32[6]{0:T(128)} %reshape.36.rows_ref, s32[6]{0:T(128)} %reshape.37.cols_ref, s32[2]{0:T(128)} %bitcast.34, f32[2,4,512,128]{3,2,1,0:T(8,128)} %copy-done.3, f32[2,4,512,128]{3,2,1,0:T(8,128)} %copy-done.4, ...), custom_call_target="tpu_custom_call" | custom-call | flops 6442450944 | bytes 12582912 | tf_op jit(solution)/shard_map/position_work/pallas_call | solution.py:176
  169.3 0.7 copy-done.10
  170.0 59.4 %exchange.4 = (f32[2,4,512,128]{3,2,1,0:T(8,128)S(1)}, f32[2,4,512,128]{3,2,1,0:T(8,128)S(1)}, f32[2,8,128]{2,1,0:T(8,128)S(1)}) custom-call(f32[2,4,512,128]{3,2,1,0:T(8,128)} %copy-done.3, f32[2,4,512,128]{3,2,1,0:T(8,128)} %copy-done.4, f32[2,4,512,128]{3,2,1,0:T(8,128)} %get-tuple-element.32.grad, f32[2,4,512,128]{3,2,1,0:T(8,128)} %get-tuple-element.33.pgrad, ...), custom_call_target="tpu_custom_call" | custom-call | flops 41943040 | bytes 12582912 | tf_op jit(solution)/shard_map/exchange/pallas_call | solution.py:435
  229.4 1.3 copy-done.5
  230.7 1.3 copy-done.6
  232.7 13.2 %position_work.6 = (f32[2,4,512,128]{3,2,1,0:T(8,128)}, f32[2,4,512,128]{3,2,1,0:T(8,128)}, f32[2,8,128]{2,1,0:T(8,128)}) custom-call(s32[6]{0:T(128)} %reshape.36.rows_ref, s32[6]{0:T(128)} %reshape.37.cols_ref, s32[2]{0:T(128)} %bitcast.35, f32[2,4,512,128]{3,2,1,0:T(8,128)} %copy-done.5, f32[2,4,512,128]{3,2,1,0:T(8,128)} %copy-done.6, ...), custom_call_target="tpu_custom_call" | custom-call | flops 6442450944 | bytes 12582912 | tf_op jit(solution)/shard_map/position_work/pallas_call | solution.py:176
  245.9 0.7 copy-done.11
  246.6 75.9 %exchange.5 = (f32[2,4,512,128]{3,2,1,0:T(8,128)S(1)}, f32[2,4,512,128]{3,2,1,0:T(8,128)S(1)}, f32[2,8,128]{2,1,0:T(8,128)S(1)}) custom-call(f32[2,4,512,128]{3,2,1,0:T(8,128)} %copy-done.5, f32[2,4,512,128]{3,2,1,0:T(8,128)} %copy-done.6, f32[2,4,512,128]{3,2,1,0:T(8,128)} %get-tuple-element.37.grad, f32[2,4,512,128]{3,2,1,0:T(8,128)} %get-tuple-element.38.pgrad, ...), custom_call_target="tpu_custom_call" | custom-call | flops 41943040 | bytes 12582912 | tf_op jit(solution)/shard_map/exchange/pallas_call | solution.py:435
  322.5 1.3 copy-done.1
  323.8 1.3 copy-done.2
  325.7 29.6 %position_work.7 = (f32[2,4,512,128]{3,2,1,0:T(8,128)}, f32[2,4,512,128]{3,2,1,0:T(8,128)}, f32[2,8,128]{2,1,0:T(8,128)}) custom-call(s32[6]{0:T(128)} %reshape.36.rows_ref, s32[6]{0:T(128)} %reshape.37.cols_ref, s32[2]{0:T(128)} %bitcast.36, f32[2,4,512,128]{3,2,1,0:T(8,128)} %copy-done.1, f32[2,4,512,128]{3,2,1,0:T(8,128)} %copy-done.2, ...), custom_call_target="tpu_custom_call" | custom-call | flops 6442450944 | bytes 12582912 | tf_op jit(solution)/shard_map/position_work/pallas_call | solution.py:176
  356.0 52.3 %exchange_last.1 = (f32[2,4,512,128]{3,2,1,0:T(8,128)S(1)}, f32[2,4,512,128]{3,2,1,0:T(8,128)S(1)}, f32[2,8,128]{2,1,0:T(8,128)S(1)}) custom-call(f32[2,4,512,128]{3,2,1,0:T(8,128)} %copy-done.1, f32[2,4,512,128]{3,2,1,0:T(8,128)} %copy-done.2, f32[2,4,512,128]{3,2,1,0:T(8,128)} %get-tuple-element.42.grad, f32[2,4,512,128]{3,2,1,0:T(8,128)} %get-tuple-element.43.pgrad, ...), custom_call_target="tpu_custom_call" | custom-call | flops 41943040 | bytes 12582912 | tf_op jit(solution)/shard_map/exchange_last/pallas_call | solution.py:435
  408.4 1.3 copy-done.7
  410.5 1.0 copy.20
  411.5 3.1 copy.25
  414.6 3.0 pad_maximum_fusion.2
  (30 shorter events, 5.1 us)
Async XLA Ops:
  0.6 27.4 %copy-start = (f32[2,4,256,256]{3,2,1,0:T(8,128)S(1)}, f32[2,4,256,256]{3,2,1,0:T(8,128)}, u32[]{:S(2)}) copy-start(f32[2,4,256,256]{3,2,1,0:T(8,128)} %param.9) | copy-start | bytes 6291460
  2.1 14.8 %collective-permute-start = (f32[2,128,256]{1,2,0:T(8,128)S(1)}, f32[2,128,256]{1,2,0:T(8,128)S(1)}, u32[]{:S(2)}, u32[]{:S(2)}) collective-permute-start(f32[2,128,256]{1,2,0:T(8,128)S(1)} %get-tuple-element.56), channel_id=1, source_target_pairs={{0,16},{16,32},{32,48},{48,64},{64,80},{80,96},{96,112},{1,17},{17... | collective-permute-start | bytes 786440 | tf_op jit(solution)/shard_map/ppermute | solution.py:475
  6.5 20.3 %copy-start.12 = (s32[1,1,2,3]{3,2,1,0:T(2,128)S(1)}, s32[1,1,2,3]{3,2,1,0:T(2,128)}, u32[]{:S(2)}) copy-start(s32[1,1,2,3]{3,2,1,0:T(2,128)} %param.10) | copy-start | bytes 76
  6.5 20.9 %copy-start.13 = (s32[1,1,2,3]{3,2,1,0:T(2,128)S(1)}, s32[1,1,2,3]{3,2,1,0:T(2,128)}, u32[]{:S(2)}) copy-start(s32[1,1,2,3]{3,2,1,0:T(2,128)} %param.11) | copy-start | bytes 76
  6.5 10.4 %collective-permute-start.1 = (f32[2,128,256]{1,2,0:T(8,128)S(1)}, f32[2,128,256]{1,2,0:T(8,128)S(1)}, u32[]{:S(2)}, u32[]{:S(2)}) collective-permute-start(f32[2,128,256]{1,2,0:T(8,128)S(1)} %get-tuple-element.57), channel_id=1, source_target_pairs={{16,0},{32,16},{48,32},{64,48},{80,64},{96,80},{112,96},{17,1},{33... | collective-permute-start | bytes 786440 | tf_op jit(solution)/shard_map/ppermute | solution.py:476
  18.0 18.8 %collective-permute-start.2 = (f32[2,512,128]{1,2,0:T(8,128)}, f32[2,512,128]{1,2,0:T(8,128)}, u32[]{:S(2)}, u32[]{:S(2)}) collective-permute-start(f32[2,512,128]{1,2,0:T(8,128)} %get-tuple-element.54), channel_id=1, source_target_pairs={{0,1},{1,2},{2,3},{3,4},{4,5},{5,6},{6,7},{7,8},{8,9},{9,10},{10,1... | collective-permute-start | bytes 1572872 | tf_op jit(solution)/shard_map/ppermute | solution.py:475
  24.8 12.3 %collective-permute-start.3 = (f32[2,512,128]{1,2,0:T(8,128)}, f32[2,512,128]{1,2,0:T(8,128)}, u32[]{:S(2)}, u32[]{:S(2)}) collective-permute-start(f32[2,512,128]{1,2,0:T(8,128)} %get-tuple-element.55), channel_id=1, source_target_pairs={{1,0},{2,1},{3,2},{4,3},{5,4},{6,5},{7,6},{8,7},{9,8},{10,9},{11,1... | collective-permute-start | bytes 1572872 | tf_op jit(solution)/shard_map/ppermute | solution.py:476
  56.0 0.7 copy-start.9
  136.4 1.3 copy-start.3
  137.7 1.3 copy-start.4
  169.3 0.7 copy-start.10
  229.4 1.3 copy-start.5
  230.7 1.3 copy-start.6
  245.9 0.7 copy-start.11
  322.4 1.3 copy-start.1
  323.8 1.3 copy-start.2
  355.3 0.7 copy-start.8
  408.3 1.3 copy-start.7

commit v3 on v2

--- a/solution.py
+++ b/solution.py
@@ -87,17 +87,18 @@
             stats[0] = stats[0] + power
             return c
 
-        lax.fori_loop(0, steps, make_exit, 0)
+        lax.fori_loop(0, steps, make_exit, 0, unroll=4)
 
         def transform(first, second):
             def left(k, c):
                 res = jnp.dot(first[...], wave[k], preferred_element_type=F32).astype(BF16)
-                at = pl.multiple_of(k * SIDE, SIDE)
+                at = k * SIDE
                 half[pl.ds(at, SIDE), 0:SIDE] = res[0:SIDE]
                 half[pl.ds(at, SIDE), SIDE:EXT] = res[SIDE:EXT]
                 return c
 
-            lax.fori_loop(0, MODES, left, 0)
+            for k in range(MODES):
+                left(k, 0)
 
             def right(k, c):
                 at = pl.multiple_of(k * 512, 512)
@@ -106,7 +107,7 @@
                 )
                 return c
 
-            lax.fori_loop(0, 2, right, 0)
+            field[...] = jnp.dot(half[...], second[...], preferred_element_type=F32)
 
         transform(left_tab, right_tab)
 
@@ -128,7 +129,7 @@
                 wave[k, pl.ds(SIDE + at, CH), :] = (parts[k][1] * factor).astype(BF16)
             return c
 
-        lax.fori_loop(0, steps, correct, 0)
+        lax.fori_loop(0, steps, correct, 0, unroll=4)
         transform(right_tab, left_tab)
 
         def spread(i, c):
@@ -162,7 +163,7 @@
                     grad[p, block + j, spot, :] = grad[p, block + j, spot, :] + adds[j]
             return c
 
-        lax.fori_loop(0, steps, spread, 0)
+        lax.fori_loop(0, steps, spread, 0, unroll=4)
         return carry
 
     lax.fori_loop(0, counts_ref[batch], visit, 0)

time: 417 us -> 374 us (0.90)
  Pallas kernels: 353 us -> 308 us
    pallas_call x4, Pallas kernels: 85.6 us -> 38.4 us  [position_work(): pl.pallas_call(functools.partial(compute_body, batch), grid=(1,), out_sha...]
where the time goes in v3:
time: 374 us; the launch traced here: 373 us
  Pallas kernels  308 us (82%)
  local copies, waits for them, and re-layouts  24.6 us (7%)
  waiting for transfers between devices  16.7 us (4%)
  starting transfers between devices  14.3 us (4%)
  other arithmetic  8.34 us (2%)
    pallas_call x4, Pallas kernels, exchange(): pl.pallas_call(functools.partial(exchange_body, last), out_shape=(jax.Sha...  270 us
    pallas_call x4, Pallas kernels, position_work(): pl.pallas_call(functools.partial(compute_body, batch), grid=(1,), out_sha...  38.4 us
    ppermute x2, waiting for transfers between devices, padded(): before = lax.ppermute(last, axis, up)  16.4 us
    unnamed x30, local copies, waits for them, and re-layouts  14.4 us
    ppermute x2, starting transfers between devices, padded(): before = lax.ppermute(last, axis, up)  11.1 us
  transfers between devices with their start and end apart: 4, of which 3 were waited for; matrix products, arithmetic and copies ran while one was open for 1% of the time, Pallas kernels for 0%

profile of v3, /device:TPU:1, one launch (start us, length us, event | category | flops | bytes accessed | tf_op | source)
XLA Modules:
  0.0 372.9 jit_solution(5207326614081178362)
XLA Ops:
  0.6 1.4 copy.13
  2.1 4.4 %collective-permute-start = (f32[2,128,256]{1,2,0:T(8,128)S(1)}, f32[2,128,256]{1,2,0:T(8,128)S(1)}, u32[]{:S(2)}, u32[]{:S(2)}) collective-permute-start(f32[2,128,256]{1,2,0:T(8,128)S(1)} %get-tuple-element.56), channel_id=1, source_target_pairs={{0,16},{16,32},{32,48},{48,64},{64,80},{80,96},{96,112},{1,17},{17... | collective-permute-start | bytes 786440 | tf_op jit(solution)/shard_map/ppermute | solution.py:476
  6.5 1.3 collective-permute-start.1
  7.8 9.1 %collective-permute-done = f32[2,128,256]{1,2,0:T(8,128)S(1)} collective-permute-done((f32[2,128,256]{1,2,0:T(8,128)S(1)}, f32[2,128,256]{1,2,0:T(8,128)S(1)}, u32[]{:S(2)}, u32[]{:S(2)}) %collective-permute-start) | collective-permute-done | bytes 262176 | tf_op jit(solution)/shard_map/ppermute | solution.py:476
  17.0 1.0 fusion
  18.0 6.8 %collective-permute-start.2 = (f32[2,512,128]{1,2,0:T(8,128)}, f32[2,512,128]{1,2,0:T(8,128)}, u32[]{:S(2)}, u32[]{:S(2)}) collective-permute-start(f32[2,512,128]{1,2,0:T(8,128)} %get-tuple-element.54), channel_id=1, source_target_pairs={{0,1},{1,2},{2,3},{3,4},{4,5},{5,6},{6,7},{7,8},{8,9},{9,10},{10,1... | collective-permute-start | bytes 1572872 | tf_op jit(solution)/shard_map/ppermute | solution.py:476
  24.8 1.9 collective-permute-start.3
  28.0 1.6 copy_bitcast_fusion.1
  29.6 7.3 %collective-permute-done.2 = f32[2,512,128]{1,2,0:T(8,128)} collective-permute-done((f32[2,512,128]{1,2,0:T(8,128)}, f32[2,512,128]{1,2,0:T(8,128)}, u32[]{:S(2)}, u32[]{:S(2)}) %collective-permute-start.2) | collective-permute-done | bytes 524320 | tf_op jit(solution)/shard_map/ppermute | solution.py:476
  37.1 2.8 pad_maximum_fusion
  39.9 2.9 copy.16
  42.8 9.5 %position_work.4 = (f32[2,4,512,128]{3,2,1,0:T(8,128)}, f32[2,4,512,128]{3,2,1,0:T(8,128)}, f32[2,8,128]{2,1,0:T(8,128)}) custom-call(s32[6]{0:T(128)} %reshape.36.rows_ref, s32[6]{0:T(128)} %reshape.37.cols_ref, s32[2]{0:T(128)} %bitcast.33, f32[2,4,512,128]{3,2,1,0:T(8,128)} %bitcast.28, f32[2,4,512,128]{3,2,1,0:T(8,128)} %bitcast.26, ...), custom_call_target="tpu_custom_call" | custom-call | flops 6442450944 | bytes 12582912 | tf_op jit(solution)/shard_map/position_work/pallas_call | solution.py:177
  52.3 0.7 copy-done.9
  53.0 71.4 %exchange.3 = (f32[2,4,512,128]{3,2,1,0:T(8,128)S(1)}, f32[2,4,512,128]{3,2,1,0:T(8,128)S(1)}, f32[2,8,128]{2,1,0:T(8,128)S(1)}) custom-call(f32[2,4,512,128]{3,2,1,0:T(8,128)} %bitcast.29, f32[2,4,512,128]{3,2,1,0:T(8,128)} %bitcast.27, f32[2,4,512,128]{3,2,1,0:T(8,128)} %get-tuple-element.27.grad, f32[2,4,512,128]{3,2,1,0:T(8,128)} %get-tuple-element.28.pgrad, ...), custom_call_target="tpu_custom_call" | custom-call | flops 41943040 | bytes 12582912 | tf_op jit(solution)/shard_map/exchange/pallas_call | solution.py:436
  124.5 1.3 copy-done.3
  125.8 1.3 copy-done.4
  127.7 9.6 %position_work.5 = (f32[2,4,512,128]{3,2,1,0:T(8,128)}, f32[2,4,512,128]{3,2,1,0:T(8,128)}, f32[2,8,128]{2,1,0:T(8,128)}) custom-call(s32[6]{0:T(128)} %reshape.36.rows_ref, s32[6]{0:T(128)} %reshape.37.cols_ref, s32[2]{0:T(128)} %bitcast.34, f32[2,4,512,128]{3,2,1,0:T(8,128)} %copy-done.3, f32[2,4,512,128]{3,2,1,0:T(8,128)} %copy-done.4, ...), custom_call_target="tpu_custom_call" | custom-call | flops 6442450944 | bytes 12582912 | tf_op jit(solution)/shard_map/position_work/pallas_call | solution.py:177
  137.3 0.7 copy-done.10
  138.0 70.9 %exchange.4 = (f32[2,4,512,128]{3,2,1,0:T(8,128)S(1)}, f32[2,4,512,128]{3,2,1,0:T(8,128)S(1)}, f32[2,8,128]{2,1,0:T(8,128)S(1)}) custom-call(f32[2,4,512,128]{3,2,1,0:T(8,128)} %copy-done.3, f32[2,4,512,128]{3,2,1,0:T(8,128)} %copy-done.4, f32[2,4,512,128]{3,2,1,0:T(8,128)} %get-tuple-element.32.grad, f32[2,4,512,128]{3,2,1,0:T(8,128)} %get-tuple-element.33.pgrad, ...), custom_call_target="tpu_custom_call" | custom-call | flops 41943040 | bytes 12582912 | tf_op jit(solution)/shard_map/exchange/pallas_call | solution.py:436
  208.9 1.3 copy-done.5
  210.2 1.3 copy-done.6
  212.2 9.7 %position_work.6 = (f32[2,4,512,128]{3,2,1,0:T(8,128)}, f32[2,4,512,128]{3,2,1,0:T(8,128)}, f32[2,8,128]{2,1,0:T(8,128)}) custom-call(s32[6]{0:T(128)} %reshape.36.rows_ref, s32[6]{0:T(128)} %reshape.37.cols_ref, s32[2]{0:T(128)} %bitcast.35, f32[2,4,512,128]{3,2,1,0:T(8,128)} %copy-done.5, f32[2,4,512,128]{3,2,1,0:T(8,128)} %copy-done.6, ...), custom_call_target="tpu_custom_call" | custom-call | flops 6442450944 | bytes 12582912 | tf_op jit(solution)/shard_map/position_work/pallas_call | solution.py:177
  222.6 66.2 %exchange.5 = (f32[2,4,512,128]{3,2,1,0:T(8,128)S(1)}, f32[2,4,512,128]{3,2,1,0:T(8,128)S(1)}, f32[2,8,128]{2,1,0:T(8,128)S(1)}) custom-call(f32[2,4,512,128]{3,2,1,0:T(8,128)} %copy-done.5, f32[2,4,512,128]{3,2,1,0:T(8,128)} %copy-done.6, f32[2,4,512,128]{3,2,1,0:T(8,128)} %get-tuple-element.37.grad, f32[2,4,512,128]{3,2,1,0:T(8,128)} %get-tuple-element.38.pgrad, ...), custom_call_target="tpu_custom_call" | custom-call | flops 41943040 | bytes 12582912 | tf_op jit(solution)/shard_map/exchange/pallas_call | solution.py:436
  288.8 1.3 copy-done.1
  290.1 1.3 copy-done.2
  292.0 9.6 %position_work.7 = (f32[2,4,512,128]{3,2,1,0:T(8,128)}, f32[2,4,512,128]{3,2,1,0:T(8,128)}, f32[2,8,128]{2,1,0:T(8,128)}) custom-call(s32[6]{0:T(128)} %reshape.36.rows_ref, s32[6]{0:T(128)} %reshape.37.cols_ref, s32[2]{0:T(128)} %bitcast.36, f32[2,4,512,128]{3,2,1,0:T(8,128)} %copy-done.1, f32[2,4,512,128]{3,2,1,0:T(8,128)} %copy-done.2, ...), custom_call_target="tpu_custom_call" | custom-call | flops 6442450944 | bytes 12582912 | tf_op jit(solution)/shard_map/position_work/pallas_call | solution.py:177
  301.6 0.7 copy-done.8
  302.3 61.3 %exchange_last.1 = (f32[2,4,512,128]{3,2,1,0:T(8,128)S(1)}, f32[2,4,512,128]{3,2,1,0:T(8,128)S(1)}, f32[2,8,128]{2,1,0:T(8,128)S(1)}) custom-call(f32[2,4,512,128]{3,2,1,0:T(8,128)} %copy-done.1, f32[2,4,512,128]{3,2,1,0:T(8,128)} %copy-done.2, f32[2,4,512,128]{3,2,1,0:T(8,128)} %get-tuple-element.42.grad, f32[2,4,512,128]{3,2,1,0:T(8,128)} %get-tuple-element.43.pgrad, ...), custom_call_target="tpu_custom_call" | custom-call | flops 41943040 | bytes 12582912 | tf_op jit(solution)/shard_map/exchange_last/pallas_call | solution.py:436
  363.6 1.3 copy-done.7
  365.8 1.0 copy.20
  366.8 3.1 copy.25
  369.9 3.0 pad_maximum_fusion.2
  (30 shorter events, 5.1 us)
Async XLA Ops:
  0.6 27.4 %copy-start = (f32[2,4,256,256]{3,2,1,0:T(8,128)S(1)}, f32[2,4,256,256]{3,2,1,0:T(8,128)}, u32[]{:S(2)}) copy-start(f32[2,4,256,256]{3,2,1,0:T(8,128)} %param.9) | copy-start | bytes 6291460
  2.1 14.8 %collective-permute-start = (f32[2,128,256]{1,2,0:T(8,128)S(1)}, f32[2,128,256]{1,2,0:T(8,128)S(1)}, u32[]{:S(2)}, u32[]{:S(2)}) collective-permute-start(f32[2,128,256]{1,2,0:T(8,128)S(1)} %get-tuple-element.56), channel_id=1, source_target_pairs={{0,16},{16,32},{32,48},{48,64},{64,80},{80,96},{96,112},{1,17},{17... | collective-permute-start | bytes 786440 | tf_op jit(solution)/shard_map/ppermute | solution.py:476
  6.5 20.3 %copy-start.12 = (s32[1,1,2,3]{3,2,1,0:T(2,128)S(1)}, s32[1,1,2,3]{3,2,1,0:T(2,128)}, u32[]{:S(2)}) copy-start(s32[1,1,2,3]{3,2,1,0:T(2,128)} %param.10) | copy-start | bytes 76
  6.5 20.9 %copy-start.13 = (s32[1,1,2,3]{3,2,1,0:T(2,128)S(1)}, s32[1,1,2,3]{3,2,1,0:T(2,128)}, u32[]{:S(2)}) copy-start(s32[1,1,2,3]{3,2,1,0:T(2,128)} %param.11) | copy-start | bytes 76
  6.5 10.4 %collective-permute-start.1 = (f32[2,128,256]{1,2,0:T(8,128)S(1)}, f32[2,128,256]{1,2,0:T(8,128)S(1)}, u32[]{:S(2)}, u32[]{:S(2)}) collective-permute-start(f32[2,128,256]{1,2,0:T(8,128)S(1)} %get-tuple-element.57), channel_id=1, source_target_pairs={{16,0},{32,16},{48,32},{64,48},{80,64},{96,80},{112,96},{17,1},{33... | collective-permute-start | bytes 786440 | tf_op jit(solution)/shard_map/ppermute | solution.py:477
  18.0 18.8 %collective-permute-start.2 = (f32[2,512,128]{1,2,0:T(8,128)}, f32[2,512,128]{1,2,0:T(8,128)}, u32[]{:S(2)}, u32[]{:S(2)}) collective-permute-start(f32[2,512,128]{1,2,0:T(8,128)} %get-tuple-element.54), channel_id=1, source_target_pairs={{0,1},{1,2},{2,3},{3,4},{4,5},{5,6},{6,7},{7,8},{8,9},{9,10},{10,1... | collective-permute-start | bytes 1572872 | tf_op jit(solution)/shard_map/ppermute | solution.py:476
  24.8 12.3 %collective-permute-start.3 = (f32[2,512,128]{1,2,0:T(8,128)}, f32[2,512,128]{1,2,0:T(8,128)}, u32[]{:S(2)}, u32[]{:S(2)}) collective-permute-start(f32[2,512,128]{1,2,0:T(8,128)} %get-tuple-element.55), channel_id=1, source_target_pairs={{1,0},{2,1},{3,2},{4,3},{5,4},{6,5},{7,6},{8,7},{9,8},{10,9},{11,1... | collective-permute-start | bytes 1572872 | tf_op jit(solution)/shard_map/ppermute | solution.py:477
  52.3 0.7 copy-start.9
  124.5 1.3 copy-start.3
  125.8 1.3 copy-start.4
  137.3 0.7 copy-start.10
  208.9 1.3 copy-start.5
  210.2 1.3 copy-start.6
  221.9 0.7 copy-start.11
  288.8 1.3 copy-start.1
  290.1 1.3 copy-start.2
  301.6 0.7 copy-start.8
  363.6 1.3 copy-start.7

commit v4 on v0

v4 whole, which is shorter than its diff:
```python
import functools
import math

import jax
import jax.numpy as jnp
import numpy as np
from jax import lax
from jax.experimental import pallas as pl
from jax.experimental.pallas import tpu as pltpu
from jax.sharding import Mesh
from jax.sharding import PartitionSpec as P

BATCHES = 2
ITERS = 2
SLOTS = 3
MODES = 4
SIDE = 256
HALF = 128
EXT = 512
UPDATES = BATCHES * ITERS
AXES = ("row_0", "row_1", "col_0", "col_1", "col_2")
ROW = ("row_0", "row_1")
COL = ("col_0", "col_1", "col_2")
F32 = jnp.float32
BF16 = jnp.bfloat16

object_rate = 0.9
probe_rate = 0.5
floor_value = 0.5
tiny_value = 1e-06


def transform_tables():
    index = np.arange(SIDE)
    angles = (index[:, None] * index[None, :] % SIDE) * (2.0 * math.pi / SIDE)
    scale = 1.0 / math.sqrt(SIDE)
    c = np.cos(angles) * scale
    s = -np.sin(angles) * scale
    left = np.block([[c, -s], [s, c]])
    return left.astype(jnp.bfloat16), left.T.astype(jnp.bfloat16)


def where_am_i():
    y, lo, x, hi, core = (lax.axis_index(name) for name in AXES)
    row, col = y * 2 + lo, x * 4 + hi * 2 + core
    z = hi * 2 + lo

    def tile(r, c):
        return (r // 2, r % 2, c // 4, (c // 2) % 2, c % 2)

    def along(axis, value):
        if axis == "x":
            return (y, lo, value, hi, core)
        if axis == "y":
            return (value, lo, x, hi, core)
        return (y, value % 2, x, value // 2, core)

    partner = (y, lo, x, hi, 1 - core)
    coords = {"x": x, "y": y, "z": z}
    return row, col, core, coords, along, partner, tile


ORDERS = (("x", "y", "z"), ("y", "x", "z"))
CH = 16
STEPS = SIDE // CH
UNROLL = 4


def fold(x):
    total = x[0:8, :]
    for i in range(1, x.shape[0] // 8):
        total = total + x[8 * i:8 * i + 8, :]
    return total


def visit(
    batch, slot, rows_ref, cols_ref, counts_ref, obj, probe, mags, left_tab, right_tab,
    terms, pgrad, stats, win, wave, half, field,
):
    lane = lax.broadcasted_iota(jnp.int32, (CH, 128), 1)
    row0 = rows_ref[batch * SLOTS + slot]
    col0 = cols_ref[batch * SLOTS + slot]
    live = jnp.where(slot < counts_ref[batch], 1.0, 0.0).astype(F32)
    block = lax.shift_right_logical(col0, 7)
    shift = col0 & 127
    back = (128 - shift) & 127
    none = jnp.zeros((8, 128), F32)

    def make_exit(i, power):
        at = pl.multiple_of(i * CH, CH)
        w = []
        keep = lane < 128 - shift
        for p in range(2):
            rolled = [
                pltpu.roll(obj[p, block + j, pl.ds(row0 + at, CH), :], back, 1) for j in range(3)
            ]
            w.append([jnp.where(keep, rolled[j], rolled[j + 1]) for j in range(2)])
        for j in range(2):
            wr, wi = w[0][j], w[1][j]
            win[0, j, pl.ds(at, CH), :] = wr
            win[1, j, pl.ds(at, CH), :] = wi
            power = power + fold(wr * wr + wi * wi)
            for k in range(MODES):
                pr = probe[0, k, pl.ds(j * SIDE + at, CH), :]
                pi = probe[1, k, pl.ds(j * SIDE + at, CH), :]
                wave[k, pl.ds(at, CH), j * 128:(j + 1) * 128] = (pr * wr - pi * wi).astype(BF16)
                wave[k, pl.ds(SIDE + at, CH), j * 128:(j + 1) * 128] = (pr * wi + pi * wr).astype(BF16)
        return power

    power = lax.fori_loop(0, STEPS, make_exit, none, unroll=UNROLL)
    stats[0] = stats[0] + live * power

    def transform(first, second):
        for k in range(MODES):
            res = jnp.dot(first[...], wave[k], preferred_element_type=F32).astype(BF16)
            half[k * SIDE:(k + 1) * SIDE, 0:SIDE] = res[0:SIDE]
            half[k * SIDE:(k + 1) * SIDE, SIDE:EXT] = res[SIDE:EXT]
        field[...] = jnp.dot(half[...], second[...], preferred_element_type=F32)

    transform(left_tab, right_tab)

    def correct(i, misfit):
        at = pl.multiple_of(i * CH, CH)
        parts = [
            (field[pl.ds(k * SIDE + at, CH), 0:SIDE], field[pl.ds(k * SIDE + at, CH), SIDE:EXT])
            for k in range(MODES)
        ]
        total = sum(re * re + im * im for re, im in parts)
        modulus = jnp.sqrt(total)
        amplitude = mags[batch, slot, pl.ds(at, CH), :]
        factor = live * (amplitude / jnp.maximum(modulus, floor_value) - 1.0)
        gap = modulus - amplitude
        gap = gap * gap
        for k in range(MODES):
            wave[k, pl.ds(at, CH), :] = (parts[k][0] * factor).astype(BF16)
            wave[k, pl.ds(SIDE + at, CH), :] = (parts[k][1] * factor).astype(BF16)
        return misfit + fold(gap[:, 0:128]) + fold(gap[:, 128:256])

    misfit = lax.fori_loop(0, STEPS, correct, none, unroll=UNROLL)
    stats[1] = stats[1] + live * misfit
    transform(right_tab, left_tab)

    def spread(i, c):
        at = pl.multiple_of(i * CH, CH)
        term = [[None, None], [None, None]]
        for j in range(2):
            wr = win[0, j, pl.ds(at, CH), :]
            wi = win[1, j, pl.ds(at, CH), :]
            tr = ti = None
            for k in range(MODES):
                ur = field[pl.ds(k * SIDE + at, CH), j * 128:(j + 1) * 128]
                ui = field[pl.ds(k * SIDE + at, CH), SIDE + j * 128:SIDE + (j + 1) * 128]
                spot = pl.ds(j * SIDE + at, CH)
                pr = probe[0, k, spot, :]
                pi = probe[1, k, spot, :]
                ar = pr * ur + pi * ui
                ai = pr * ui - pi * ur
                tr = ar if tr is None else tr + ar
                ti = ai if ti is None else ti + ai
                pgrad[0, k, spot, :] = pgrad[0, k, spot, :] + (wr * ur + wi * ui)
                pgrad[1, k, spot, :] = pgrad[1, k, spot, :] + (wr * ui - wi * ur)
            term[0][j], term[1][j] = tr, ti
        low = lane < shift
        zero = jnp.zeros((CH, 128), F32)
        spot = pl.ds(SIDE + at, CH)
        for p in range(2):
            a = pltpu.roll(term[p][0], shift, 1)
            b = pltpu.roll(term[p][1], shift, 1)
            terms[slot, p, 1, spot, :] = jnp.where(low, zero, a)
            terms[slot, p, 2, spot, :] = jnp.where(low, a, b)
            terms[slot, p, 3, spot, :] = jnp.where(low, b, zero)
        return c

    lax.fori_loop(0, STEPS, spread, 0, unroll=UNROLL)


def body(
    rows_ref, cols_ref, counts_ref, object_in, probe_in, mags_in, left_in, right_in,
    object_out, probe_out, errors,
    obj, probes, grad, pgrad, terms, stats, mags, left_tab, right_tab, win, wave, half, field,
    core_in, acc, one_in, one, two_in, z_in, tile_in, tile_z, tile_core,
    col_in, row_in, mid, rdma_send, rdma_recv, local, ready,
):
    row, col, core, coords, along, partner, tile = where_am_i()
    up, down = tile((row + 7) % 8, col), tile((row + 1) % 8, col)
    left, right = tile(row, (col + 15) % 16), tile(row, (col + 1) % 16)
    has_left, has_right, has_up, has_down = col > 0, col < 15, row > 0, row < 7
    greeted = [partner, up, down, left, right]
    for axis in ("x", "y", "z"):
        for d in (1, 2, 3):
            greeted.append(along(axis, (coords[axis] + d) % 4))

    def greet(sem):
        for peer in greeted:
            pl.semaphore_signal(sem, inc=1, device_id=peer, device_id_type=pl.DeviceIdType.MESH)

    barrier = pltpu.get_barrier_semaphore()
    greet(barrier)

    loads = []

    def load(src, dst):
        copy = pltpu.make_async_copy(src, dst, local.at[len(loads)])
        copy.start()
        loads.append(copy)

    for j in range(2):
        load(object_in.at[:, :, j * 128:(j + 1) * 128], obj.at[:, 1 + j, HALF:HALF + SIDE, :])
    for j in range(2):
        load(
            probe_in.at[:, :, :, j * 128:(j + 1) * 128],
            probes.at[0, :, :, j * SIDE:(j + 1) * SIDE, :],
        )
    load(left_in, left_tab)
    load(right_in, right_tab)
    load(mags_in.at[0, 0], mags)

    count = [0]

    def message(src, dst, peer):
        n = count[0]
        count[0] += 1
        return pltpu.make_async_remote_copy(
            src_ref=src, dst_ref=dst, send_sem=rdma_send.at[n], recv_sem=rdma_recv.at[n],
            device_id=peer, device_id_type=pl.DeviceIdType.MESH,
        )

    def send(src, dst, peer):
        copy = message(src, dst, peer)
        copy.start()
        return copy

    def wait(copies):
        for copy in copies:
            copy.wait()

    def halo_messages(p):
        return [
            message(obj.at[p, 2], col_in.at[2, p], right),
            message(obj.at[p, 1], col_in.at[3, p], left),
        ]

    def take_halo():
        for p in range(2):
            obj[p, 0] = jnp.where(has_left, col_in[2, p], 0.0)
            obj[p, 3] = jnp.where(has_right, col_in[3, p], 0.0)

    pl.semaphore_wait(barrier, len(greeted))
    wait(loads[0:2])
    first = [
        send(obj.at[:, 1:3, HALF:SIDE, :], row_in.at[1, :, :, 0:HALF, :], up),
        send(obj.at[:, 1:3, SIDE:SIDE + HALF, :], row_in.at[0, :, :, 0:HALF, :], down),
    ]

    def clear(i, c):
        at = pl.multiple_of(i * 64, 64)
        nothing = jnp.zeros((64, 128), F32)
        for s in range(SLOTS):
            for p in range(2):
                for b in range(5):
                    terms[s, p, b, pl.ds(at, 64), :] = nothing
        return c

    lax.fori_loop(0, 12, clear, 0)
    pgrad[...] = jnp.zeros_like(pgrad)
    wait(first)
    for p in range(2):
        for j in range(2):
            obj[p, 1 + j, 0:HALF, :] = jnp.where(has_up, row_in[0, p, j, 0:HALF, :], 0.0)
            obj[p, 1 + j, SIDE + HALF:EXT, :] = jnp.where(has_down, row_in[1, p, j, 0:HALF, :], 0.0)
    halo = halo_messages(0) + halo_messages(1)
    for copy in halo:
        copy.start()
    wait(halo)
    take_halo()
    greet(ready)
    wait(loads[2:7])

    base = count[0]

    def update(u, carry):
        count[0] = base
        batch = u % BATCHES
        now = u % 2
        probe, fresh = probes.at[now], probes.at[1 - now]
        stats[...] = jnp.zeros_like(stats)

        def one_slot(slot, c):
            visit(
                batch, slot, rows_ref, cols_ref, counts_ref, obj, probe, mags, left_tab, right_tab,
                terms, pgrad, stats, win, wave, half, field,
            )
            return c

        lax.fori_loop(0, SLOTS, one_slot, 0)

        spots = []
        for s in range(SLOTS):
            row0 = rows_ref[batch * SLOTS + s]
            col0 = cols_ref[batch * SLOTS + s]
            spots.append((1 - lax.shift_right_logical(col0, 7), SIDE - row0))

        def add_terms(p, b):
            def chunk(i, c):
                at = pl.multiple_of(i * 32, 32)
                grad[p, b, pl.ds(at, 32), :] = sum(
                    terms[s, p, spots[s][0] + b, pl.ds(spots[s][1] + at, 32), :] for s in range(SLOTS)
                )
                return c

            lax.fori_loop(0, EXT // 32, chunk, 0, unroll=4)

        pl.semaphore_wait(ready, len(greeted))

        core_sent = [
            send(stats, tile_core, partner),
            send(pgrad.at[1 - core], core_in, partner),
        ]
        cols_sent = []
        for p in range(2):
            add_terms(p, 3)
            cols = [send(grad.at[p, 3], col_in.at[0, p], right)]
            add_terms(p, 0)
            cols.append(send(grad.at[p, 0], col_in.at[1, p], left))
            cols_sent.append(cols)

        def scatter(phase, source, landing, length, tile_value):
            me = coords[ORDERS[0][phase]]
            tile_in[phase, me] = tile_value
            slot = tile_in.at[phase, me]
            sent = []
            for d in (2, 1, 3):
                sent.append(send(slot, slot, along(ORDERS[0][phase], (me + d) % 4)))
                for g in range(2):
                    axis = ORDERS[g][phase]
                    to = (coords[axis] + d) % 4
                    at = pl.multiple_of(to * length, length)
                    sent.append(
                        send(
                            source.at[2 * g:2 * g + 2, pl.ds(at, length), :],
                            landing.at[d - 1, 2 * g:2 * g + 2],
                            along(axis, to),
                        )
                    )
            return sent

        def gather_sum(phase, source, landing, length):
            out = []
            for g in range(2):
                at = pl.multiple_of(coords[ORDERS[g][phase]] * length, length)
                for k in (2 * g, 2 * g + 1):
                    out.append(
                        source[k, pl.ds(at, length), :] + landing[0, k] + landing[1, k] + landing[2, k]
                    )
            return out

        def tile_total(phase):
            return (tile_in[phase, 0] + tile_in[phase, 1]) + (tile_in[phase, 2] + tile_in[phase, 3])

        def send_rows(p, j):
            return [
                send(mid.at[p, j, 0:SIDE, :], row_in.at[1, p, j], up),
                send(mid.at[p, j, SIDE:EXT, :], row_in.at[0, p, j], down),
            ]

        def make_mid(p):
            wait(cols_sent[p])
            mid[p, 0] = grad[p, 1] + jnp.where(has_left, col_in[0, p], 0.0)
            mid[p, 1] = grad[p, 2] + jnp.where(has_right, col_in[1, p], 0.0)

        wait(core_sent)
        for k in range(MODES):
            acc[k] = pgrad[core, k] + core_in[k]
        sent = scatter(0, acc, one_in, 128, stats[...] + tile_core[...])

        def peak_step(i, best):
            at = pl.multiple_of(i * 16, 16)
            total = None
            for p in range(2):
                for k in range(MODES):
                    v = probe[p, k, pl.ds(at, 16), :]
                    total = v * v if total is None else total + v * v
            return jnp.maximum(best, jnp.maximum(total[0:8], total[8:16]))

        best = lax.fori_loop(0, EXT // 16, peak_step, jnp.zeros((8, 128), F32), unroll=4)
        rate = object_rate / (jnp.max(best) + tiny_value)

        def update_object(p, j):
            upper = jnp.where(has_up, row_in[0, p, j], 0.0)
            lower = jnp.where(has_down, row_in[1, p, j], 0.0)
            top = mid[p, j, 0:SIDE, :] + upper
            low = mid[p, j, SIDE:EXT, :] + lower
            rate_up = jnp.where(has_up, rate, 0.0)
            rate_down = jnp.where(has_down, rate, 0.0)
            b = 1 + j
            obj[p, b, 0:HALF, :] = obj[p, b, 0:HALF, :] + rate_up * top[0:HALF]
            obj[p, b, HALF:SIDE, :] = obj[p, b, HALF:SIDE, :] + rate * top[HALF:SIDE]
            obj[p, b, SIDE:SIDE + HALF, :] = obj[p, b, SIDE:SIDE + HALF, :] + rate * low[0:HALF]
            obj[p, b, SIDE + HALF:EXT, :] = obj[p, b, SIDE + HALF:EXT, :] + rate_down * low[HALF:SIDE]

        for p in range(2):
            add_terms(p, 1)
            add_terms(p, 2)
        make_mid(0)
        rows_sent = [send_rows(0, 0), send_rows(0, 1)]

        wait(sent)
        for k, v in enumerate(gather_sum(0, acc, one_in, 128)):
            one[k] = v
        sent = scatter(1, one, two_in, 32, tile_total(0))

        make_mid(1)

        wait(sent)
        z = coords["z"]
        for k, v in enumerate(gather_sum(1, one, two_in, 32)):
            z_in[z, k] = v
        tile_z[z] = tile_total(1)
        sent = []
        for d in (2, 1, 3):
            peer = along("z", (z + d) % 4)
            sent.append(send(tile_z.at[z], tile_z.at[z], peer))
            sent.append(send(z_in.at[z], z_in.at[z], peer))
        rows_sent.append(send_rows(1, 0))
        pgrad[...] = jnp.zeros_like(pgrad)
        wait(sent)

        totals = (tile_z[0] + tile_z[1]) + (tile_z[2] + tile_z[3])
        errors[u] = totals[1]
        gain = probe_rate * SIDE * SIDE / jnp.sum(totals[0])
        starts = []
        for g in range(2):
            a, b = coords[ORDERS[g][0]], coords[ORDERS[g][1]]
            starts.append((a * 128, a * 128 + b * 32))
        for k in range(MODES):
            spot = pl.ds(pl.multiple_of(starts[k // 2][1], 32), 32)
            total = (z_in[0, k] + z_in[1, k]) + (z_in[2, k] + z_in[3, k])
            fresh[core, k, spot, :] = probe[core, k, spot, :] + gain * total

        def block_of(g, at, length):
            at = pl.multiple_of(at, length)
            return fresh.at[core, 2 * g:2 * g + 2, pl.ds(at, length), :]

        def spread(phase, length):
            out = {}
            for d in (2, 1, 3):
                for g in range(2):
                    axis = ORDERS[g][phase]
                    block = block_of(g, starts[g][phase], length)
                    out[d, g] = send(block, block, along(axis, (coords[axis] + d) % 4))
            return out

        out2 = spread(1, 32)
        rows_sent.append(send_rows(1, 1))
        wait(out2.values())
        out1 = spread(0, 128)
        to_core = []
        for g in range(2):
            block = block_of(g, starts[g][0], 128)
            to_core.append(send(block, block, partner))

        halo = halo_messages(0) + halo_messages(1)
        wait(rows_sent[0] + rows_sent[1])
        for j in range(2):
            update_object(0, j)

        @pl.when(u < UPDATES - 1)
        def _():
            halo[0].start()
            halo[1].start()

        for d in (1, 3, 2):
            for g in range(2):
                out1[d, g].wait()
                axis = ORDERS[g][0]
                block = block_of(g, (coords[axis] + 4 - d) % 4 * 128, 128)
                to_core.append(send(block, block, partner))

        wait(rows_sent[2] + rows_sent[3])
        for j in range(2):
            update_object(1, j)

        @pl.when(u < UPDATES - 1)
        def _():
            halo[2].start()
            halo[3].start()

        wait(to_core)

        @pl.when(u < UPDATES - 1)
        def _():
            wait(halo)
            take_halo()
            greet(ready)

        return carry

    lax.fori_loop(0, UPDATES, update, 0)

    stores = []
    for j in range(2):
        stores.append(
            pltpu.make_async_copy(
                obj.at[:, 1 + j, HALF:HALF + SIDE, :], object_out.at[:, :, j * 128:(j + 1) * 128], local.at[j]
            )
        )
        stores.append(
            pltpu.make_async_copy(
                probes.at[UPDATES % 2, :, :, j * SIDE:(j + 1) * SIDE, :],
                probe_out.at[:, :, :, j * 128:(j + 1) * 128],
                local.at[2 + j],
            )
        )
    for copy in stores:
        copy.start()
    wait(stores)


def on_device(object_field, probe, pos_rows, pos_cols, counts, magnitudes):
    tables = tuple(jnp.asarray(t) for t in transform_tables())
    anywhere = pl.BlockSpec(memory_space=pl.ANY)
    whole = pl.BlockSpec(memory_space=pltpu.VMEM)
    smem = pl.BlockSpec(memory_space=pltpu.SMEM)
    messages = 80
    out, probe_out, errors = pl.pallas_call(
        body,
        out_shape=(
            jax.ShapeDtypeStruct((2, SIDE, SIDE), F32),
            jax.ShapeDtypeStruct((2, MODES, SIDE, SIDE), F32),
            jax.ShapeDtypeStruct((UPDATES, 8, 128), F32),
        ),
        in_specs=[smem, smem, smem] + [anywhere] * 5,
        out_specs=(anywhere, anywhere, whole),
        scratch_shapes=[
            pltpu.VMEM((2, 4, EXT, 128), F32),
            pltpu.VMEM((2, 2, MODES, EXT, 128), F32),
            pltpu.VMEM((2, 4, EXT, 128), F32),
            pltpu.VMEM((2, MODES, EXT, 128), F32),
            pltpu.VMEM((SLOTS, 2, 5, 3 * SIDE, 128), F32),
            pltpu.VMEM((2, 8, 128), F32),
            pltpu.VMEM((BATCHES, SLOTS, SIDE, SIDE), F32),
            pltpu.VMEM((EXT, EXT), BF16),
            pltpu.VMEM((EXT, EXT), BF16),
            pltpu.VMEM((2, 2, SIDE, 128), F32),
            pltpu.VMEM((MODES, EXT, SIDE), BF16),
            pltpu.VMEM((MODES * SIDE, EXT), BF16),
            pltpu.VMEM((MODES * SIDE, EXT), F32),
            pltpu.VMEM((MODES, EXT, 128), F32),
            pltpu.VMEM((MODES, EXT, 128), F32),
            pltpu.VMEM((3, MODES, 128, 128), F32),
            pltpu.VMEM((MODES, 128, 128), F32),
            pltpu.VMEM((3, MODES, 32, 128), F32),
            pltpu.VMEM((4, MODES, 32, 128), F32),
            pltpu.VMEM((2, 4, 2, 8, 128), F32),
            pltpu.VMEM((4, 2, 8, 128), F32),
            pltpu.VMEM((2, 8, 128), F32),
            pltpu.VMEM((4, 2, EXT, 128), F32),
            pltpu.VMEM((2, 2, 2, SIDE, 128), F32),
            pltpu.VMEM((2, 2, EXT, 128), F32),
            pltpu.SemaphoreType.DMA((messages,)),
            pltpu.SemaphoreType.DMA((messages,)),
            pltpu.SemaphoreType.DMA((8,)),
            pltpu.SemaphoreType.REGULAR,
        ],
        cost_estimate=pl.CostEstimate(flops=80 << 30, bytes_accessed=12 << 20, transcendentals=0),
        compiler_params=pltpu.CompilerParams(
            collective_id=0, has_side_effects=True, vmem_limit_bytes=60 << 20
        ),
        name="whole_sweep",
    )(
        pos_rows.reshape(-1), pos_cols.reshape(-1), counts.reshape(-1),
        object_field, probe, magnitudes, *tables,
    )
    return (out, probe_out, jnp.sum(errors, axis=(1, 2)))


def solution(mesh):
    finer = Mesh(mesh.devices.reshape(4, 2, 4, 2, 2), AXES)
    return jax.shard_map(
        on_device,
        mesh=finer,
        in_specs=(
            P(None, ROW, COL),
            P(),
            P(ROW, COL, None, None),
            P(ROW, COL, None, None),
            P(ROW, COL, None),
            P(ROW, COL, None, None, None, None),
        ),
        out_specs=(P(None, ROW, COL), P(), P()),
        check_vma=False,
    )
```

time: 1270 us -> 302 us (0.24); the launches traced: 1260 us -> 302 us
  blocking collectives: 392 us -> 0 us
  waiting for transfers between devices: 321 us -> 0 us
  Pallas kernels: 0 us -> 293 us
  starting transfers between devices: 231 us -> 0 us
  local copies, waits for them, and re-layouts: 110 us -> 7.45 us
  other arithmetic: 94.6 us -> 1.34 us
  matrix products: 51.3 us -> 0 us
  loops' own time: 35.8 us -> 0 us
  between operations: 20.5 us -> 0.64 us
    psum x9 -> x0, blocking collectives: 392 us -> none  [the longest x4 321 us: on_device(): summed, power_total = lax.psum((probe_grad, power_sum), ROW_COL)]
    pallas_call x0 -> x1, Pallas kernels: none -> 293 us  [on_device(): pl.pallas_call(body, out_shape=(jax.ShapeDtypeStruct((2, SIDE, SIDE), F32...]
    ppermute x32 -> x0, starting transfers between devices: 231 us -> none  [the longest x16 175 us: shifted(): lax.ppermute(value, axis, [(source, source + steps) for source in range(l...]
    psum x4 -> x0, waiting for transfers between devices: 205 us -> none  [on_device(): summed, power_total = lax.psum((probe_grad, power_sum), ROW_COL)]
    ppermute x32 -> x0, waiting for transfers between devices: 116 us -> none  [the longest x16 69.4 us: shifted(): lax.ppermute(value, axis, [(source, source + steps) for source in range(l...]
    dot_general x12 -> x0, matrix products: 51.3 us -> none  [transform(): jnp.einsum('imxb,oiby->omxy', left_half, table, preferred_element_type=jn...]
    dynamic_update_slice x6 -> x0, local copies, waits for them, and re-layouts: 39.3 us -> none  [visit(): lax.dynamic_update_slice(object_grad, region + object_term, anchor)]
    add x23 -> x0, other arithmetic: 36.3 us -> none  [the longest x6 14.2 us: visit(): region + object_term]
  transfers between devices with their start and end apart: 36 -> 0, of which waited for: 22 -> 0; matrix products, arithmetic and copies ran while one was open for 4% -> 0% of each run, Pallas kernels for 0% -> 0%
where the time goes in v4:
time: 302 us
  Pallas kernels  293 us (97%)
  local copies, waits for them, and re-layouts  7.45 us (2%)
    pallas_call x1, Pallas kernels, on_device(): pl.pallas_call(body, out_shape=(jax.ShapeDtypeStruct((2, SIDE, SIDE), F32...  293 us

profile of v4, /device:TPU:1, one launch (start us, length us, event | category | flops | bytes accessed | tf_op | source)
XLA Modules:
  0.0 302.1 jit_solution(12420913007380602544)
XLA Ops:
  0.6 1.3 reshape.15.rows_ref
  1.9 1.3 reshape.16.cols_ref
  3.2 292.6 %whole_sweep.1 = (f32[2,256,256]{2,1,0:T(8,128)}, f32[2,4,256,256]{3,2,1,0:T(8,128)}, f32[4,8,128]{2,1,0:T(8,128)}) custom-call(s32[6]{0:T(128)} %reshape.15.rows_ref, s32[6]{0:T(128)} %reshape.16.cols_ref, s32[2]{0:T(128)} %bitcast.1, f32[2,256,256]{2,1,0:T(8,128)} %object_in.1, f32[2,4,256,256]{3,2,1,0:T(8,128)} %probe_in.1, ...), custom_call_target="tpu_custom_call" | custom-call | flops 85899345920 | bytes 12582912 | tf_op jit(solution)/shard_map/whole_sweep/pallas_call | solution.py:525
  295.8 1.3 reduce_sum.9
  297.2 1.9 copy.13
  299.0 3.0 %copy.14 = f32[2,4,256,256]{3,2,1,0:T(8,128)} copy(f32[2,4,256,256]{3,2,1,0:T(8,128)} %get-tuple-element.13) | data formatting | bytes 4194304

commit v5 on v4

--- a/solution.py
+++ b/solution.py
@@ -78,9 +78,9 @@
     terms, pgrad, stats, win, wave, half, field,
 ):
     lane = lax.broadcasted_iota(jnp.int32, (CH, 128), 1)
-    row0 = rows_ref[batch * SLOTS + slot]
-    col0 = cols_ref[batch * SLOTS + slot]
-    live = jnp.where(slot < counts_ref[batch], 1.0, 0.0).astype(F32)
+    row0 = rows_ref[0, 0, batch, slot]
+    col0 = cols_ref[0, 0, batch, slot]
+    live = jnp.where(slot < counts_ref[0, 0, batch], 1.0, 0.0).astype(F32)
     block = lax.shift_right_logical(col0, 7)
     shift = col0 & 127
     back = (128 - shift) & 127
@@ -236,21 +236,47 @@
 
     def halo_messages(p):
         return [
-            message(obj.at[p, 2], col_in.at[2, p], right),
-            message(obj.at[p, 1], col_in.at[3, p], left),
+            message(obj.at[p, 2], obj.at[p, 0], right),
+            message(obj.at[p, 1], obj.at[p, 3], left),
         ]
 
-    def take_halo():
-        for p in range(2):
-            obj[p, 0] = jnp.where(has_left, col_in[2, p], 0.0)
-            obj[p, 3] = jnp.where(has_right, col_in[3, p], 0.0)
+    def start_halo(pair):
+        @pl.when(has_right)
+        def _():
+            pair[0].start()
+
+        @pl.when(has_left)
+        def _():
+            pair[1].start()
+
+    def wait_halo(pair):
+        @pl.when(has_right)
+        def _():
+            pair[0].wait_send()
+            pair[1].wait_recv()
+
+        @pl.when(has_left)
+        def _():
+            pair[1].wait_send()
+            pair[0].wait_recv()
 
     pl.semaphore_wait(barrier, len(greeted))
     wait(loads[0:2])
     first = [
-        send(obj.at[:, 1:3, HALF:SIDE, :], row_in.at[1, :, :, 0:HALF, :], up),
-        send(obj.at[:, 1:3, SIDE:SIDE + HALF, :], row_in.at[0, :, :, 0:HALF, :], down),
+        [
+            send(obj.at[p, 1:3, HALF:SIDE, :], row_in.at[1, p, :, 0:HALF, :], up),
+            send(obj.at[p, 1:3, SIDE:SIDE + HALF, :], row_in.at[0, p, :, 0:HALF, :], down),
+        ]
+        for p in range(2)
     ]
+
+    @pl.when(jnp.logical_not(has_left))
+    def _():
+        obj[:, 0] = jnp.zeros((2, EXT, 128), F32)
+
+    @pl.when(jnp.logical_not(has_right))
+    def _():
+        obj[:, 3] = jnp.zeros((2, EXT, 128), F32)
 
     def clear(i, c):
         at = pl.multiple_of(i * 64, 64)
@@ -263,16 +289,15 @@
 
     lax.fori_loop(0, 12, clear, 0)
     pgrad[...] = jnp.zeros_like(pgrad)
-    wait(first)
+    halo = [halo_messages(p) for p in range(2)]
     for p in range(2):
+        wait(first[p])
         for j in range(2):
             obj[p, 1 + j, 0:HALF, :] = jnp.where(has_up, row_in[0, p, j, 0:HALF, :], 0.0)
             obj[p, 1 + j, SIDE + HALF:EXT, :] = jnp.where(has_down, row_in[1, p, j, 0:HALF, :], 0.0)
-    halo = halo_messages(0) + halo_messages(1)
-    for copy in halo:
-        copy.start()
-    wait(halo)
-    take_halo()
+        start_halo(halo[p])
+    for p in range(2):
+        wait_halo(halo[p])
     greet(ready)
     wait(loads[2:7])
 
@@ -296,8 +321,8 @@
 
         spots = []
         for s in range(SLOTS):
-            row0 = rows_ref[batch * SLOTS + s]
-            col0 = cols_ref[batch * SLOTS + s]
+            row0 = rows_ref[0, 0, batch, s]
+            col0 = cols_ref[0, 0, batch, s]
             spots.append((1 - lax.shift_right_logical(col0, 7), SIDE - row0))
 
         def add_terms(p, b):
@@ -358,10 +383,30 @@
             return (tile_in[phase, 0] + tile_in[phase, 1]) + (tile_in[phase, 2] + tile_in[phase, 3])
 
         def send_rows(p, j):
-            return [
-                send(mid.at[p, j, 0:SIDE, :], row_in.at[1, p, j], up),
-                send(mid.at[p, j, SIDE:EXT, :], row_in.at[0, p, j], down),
+            outer = [
+                send(mid.at[p, j, 0:HALF, :], row_in.at[1, p, j, 0:HALF], up),
+                send(mid.at[p, j, SIDE + HALF:EXT, :], row_in.at[0, p, j, HALF:SIDE], down),
             ]
+            inner = [
+                message(mid.at[p, j, HALF:SIDE, :], row_in.at[1, p, j, HALF:SIDE], up),
+                message(mid.at[p, j, SIDE:SIDE + HALF, :], row_in.at[0, p, j, 0:HALF], down),
+            ]
+
+            @pl.when(u < UPDATES - 1)
+            def _():
+                inner[0].start()
+                inner[1].start()
+
+            return (outer, inner)
+
+        def wait_rows(pair):
+            for outer, inner in pair:
+                wait(outer)
+
+            @pl.when(u < UPDATES - 1)
+            def _():
+                for outer, inner in pair:
+                    wait(inner)
 
         def make_mid(p):
             wait(cols_sent[p])
@@ -421,8 +466,8 @@
             peer = along("z", (z + d) % 4)
             sent.append(send(tile_z.at[z], tile_z.at[z], peer))
             sent.append(send(z_in.at[z], z_in.at[z], peer))
+        pgrad[...] = jnp.zeros_like(pgrad)
         rows_sent.append(send_rows(1, 0))
-        pgrad[...] = jnp.zeros_like(pgrad)
         wait(sent)
 
         totals = (tile_z[0] + tile_z[1]) + (tile_z[2] + tile_z[3])
@@ -452,22 +497,24 @@
 
         out2 = spread(1, 32)
         rows_sent.append(send_rows(1, 1))
+        halo = [halo_messages(p) for p in range(2)]
+
+        def finish_object(p):
+            wait_rows(rows_sent[2 * p:2 * p + 2])
+            for j in range(2):
+                update_object(p, j)
+
+            @pl.when(u < UPDATES - 1)
+            def _():
+                start_halo(halo[p])
+
         wait(out2.values())
         out1 = spread(0, 128)
+        finish_object(0)
         to_core = []
         for g in range(2):
             block = block_of(g, starts[g][0], 128)
             to_core.append(send(block, block, partner))
-
-        halo = halo_messages(0) + halo_messages(1)
-        wait(rows_sent[0] + rows_sent[1])
-        for j in range(2):
-            update_object(0, j)
-
-        @pl.when(u < UPDATES - 1)
-        def _():
-            halo[0].start()
-            halo[1].start()
 
         for d in (1, 3, 2):
             for g in range(2):
@@ -476,21 +523,13 @@
                 block = block_of(g, (coords[axis] + 4 - d) % 4 * 128, 128)
                 to_core.append(send(block, block, partner))
 
-        wait(rows_sent[2] + rows_sent[3])
-        for j in range(2):
-            update_object(1, j)
+        finish_object(1)
+        wait(to_core)
 
         @pl.when(u < UPDATES - 1)
         def _():
-            halo[2].start()
-            halo[3].start()
-
-        wait(to_core)
-
-        @pl.when(u < UPDATES - 1)
-        def _():
-            wait(halo)
-            take_halo()
+            for p in range(2):
+                wait_halo(halo[p])
             greet(ready)
 
         return carry
@@ -521,7 +560,7 @@
     anywhere = pl.BlockSpec(memory_space=pl.ANY)
     whole = pl.BlockSpec(memory_space=pltpu.VMEM)
     smem = pl.BlockSpec(memory_space=pltpu.SMEM)
-    messages = 80
+    messages = 96
     out, probe_out, errors = pl.pallas_call(
         body,
         out_shape=(
@@ -554,7 +593,7 @@
             pltpu.VMEM((2, 4, 2, 8, 128), F32),
             pltpu.VMEM((4, 2, 8, 128), F32),
             pltpu.VMEM((2, 8, 128), F32),
-            pltpu.VMEM((4, 2, EXT, 128), F32),
+            pltpu.VMEM((2, 2, EXT, 128), F32),
             pltpu.VMEM((2, 2, 2, SIDE, 128), F32),
             pltpu.VMEM((2, 2, EXT, 128), F32),
             pltpu.SemaphoreType.DMA((messages,)),
@@ -568,7 +607,7 @@
         ),
         name="whole_sweep",
     )(
-        pos_rows.reshape(-1), pos_cols.reshape(-1), counts.reshape(-1),
+        pos_rows, pos_cols, counts,
         object_field, probe, magnitudes, *tables,
     )
     return (out, probe_out, jnp.sum(errors, axis=(1, 2)))

time: 302 us -> 292 us (0.967)
  Pallas kernels: 293 us -> 284 us
    pallas_call x1, Pallas kernels: 293 us -> 284 us  [on_device(): pl.pallas_call(body, out_shape=(jax.ShapeDtypeStruct((2, SIDE, SIDE), F32...]
where the time goes in v5:
time: 292 us; the launch traced here: 291 us
  Pallas kernels  284 us (97%)
  local copies, waits for them, and re-layouts  4.91 us (2%)
    pallas_call x1, Pallas kernels, on_device(): pl.pallas_call(body, out_shape=(jax.ShapeDtypeStruct((2, SIDE, SIDE), F32...  284 us

profile of v5, /device:TPU:1, one launch (start us, length us, event | category | flops | bytes accessed | tf_op | source)
XLA Modules:
  0.0 291.2 jit_solution(4918422510964183737)
XLA Ops:
  0.6 284.3 %whole_sweep.1 = (f32[2,256,256]{2,1,0:T(8,128)}, f32[2,4,256,256]{3,2,1,0:T(8,128)}, f32[4,8,128]{2,1,0:T(8,128)}) custom-call(s32[1,1,2,3]{3,2,1,0:T(2,128)} %rows_ref.1, s32[1,1,2,3]{3,2,1,0:T(2,128)} %cols_ref.1, s32[1,1,2]{2,1,0:T(1,128)} %counts_ref.1, f32[2,256,256]{2,1,0:T(8,128)} %object_in.1, f32[2,4,256,256]{3,2,1,0:T(8,128)} %probe_in.1, ...), custom_call_target="tpu_custom_call" | custom-call | flops 85899345920 | bytes 12582912 | tf_op jit(solution)/shard_map/whole_sweep/pallas_call | solution.py:564
  284.9 1.3 reduce_sum.9
  286.3 1.9 copy.13
  288.1 3.0 %copy.14 = f32[2,4,256,256]{3,2,1,0:T(8,128)} copy(f32[2,4,256,256]{3,2,1,0:T(8,128)} %get-tuple-element.13) | data formatting | bytes 4194304

commit v6 on v5

--- a/solution.py
+++ b/solution.py
@@ -36,8 +36,20 @@
     scale = 1.0 / math.sqrt(SIDE)
     c = np.cos(angles) * scale
     s = -np.sin(angles) * scale
-    left = np.block([[c, -s], [s, c]])
-    return left.astype(jnp.bfloat16), left.T.astype(jnp.bfloat16)
+    near = np.arange(HALF)
+    tables = []
+    for parity in range(2):
+        pick = np.arange(parity, SIDE, 2)
+        cr, sr = c[np.ix_(pick, near)], s[np.ix_(pick, near)]
+        tables.append(np.block([[cr, -sr], [sr, cr]]))
+    for parity in range(2):
+        pick = np.arange(parity, SIDE, 2)
+        cr, sr = c[np.ix_(near, pick)], s[np.ix_(near, pick)]
+        tables.append(np.block([[cr, sr], [-sr, cr]]))
+    tables = tables + [t.T for t in tables]
+    order = np.concatenate([np.arange(0, SIDE, 2), np.arange(1, SIDE, 2)])
+    sort = np.eye(SIDE)[order]
+    return (np.stack(tables).astype(jnp.bfloat16), np.stack([sort, sort.T]).astype(jnp.bfloat16))
 
 
 def where_am_i():
@@ -74,7 +86,7 @@
 
 
 def visit(
-    batch, slot, rows_ref, cols_ref, counts_ref, obj, probe, mags, left_tab, right_tab,
+    batch, slot, rows_ref, cols_ref, counts_ref, obj, probe, mags, tables,
     terms, pgrad, stats, win, wave, half, field,
 ):
     lane = lax.broadcasted_iota(jnp.int32, (CH, 128), 1)
@@ -88,57 +100,87 @@
 
     def make_exit(i, power):
         at = pl.multiple_of(i * CH, CH)
+        keep = lane < 128 - shift
         w = []
-        keep = lane < 128 - shift
-        for p in range(2):
-            rolled = [
-                pltpu.roll(obj[p, block + j, pl.ds(row0 + at, CH), :], back, 1) for j in range(3)
-            ]
-            w.append([jnp.where(keep, rolled[j], rolled[j + 1]) for j in range(2)])
+        for h in range(2):
+            for p in range(2):
+                rolled = [
+                    pltpu.roll(obj[p, block + j, pl.ds(row0 + h * HALF + at, CH), :], back, 1)
+                    for j in range(3)
+                ]
+                w.append([jnp.where(keep, rolled[j], rolled[j + 1]) for j in range(2)])
         for j in range(2):
-            wr, wi = w[0][j], w[1][j]
-            win[0, j, pl.ds(at, CH), :] = wr
-            win[1, j, pl.ds(at, CH), :] = wi
-            power = power + fold(wr * wr + wi * wi)
+            for h in range(2):
+                wr, wi = w[2 * h][j], w[2 * h + 1][j]
+                win[0, j, pl.ds(h * HALF + at, CH), :] = wr
+                win[1, j, pl.ds(h * HALF + at, CH), :] = wi
+                power = power + fold(wr * wr + wi * wi)
             for k in range(MODES):
-                pr = probe[0, k, pl.ds(j * SIDE + at, CH), :]
-                pi = probe[1, k, pl.ds(j * SIDE + at, CH), :]
-                wave[k, pl.ds(at, CH), j * 128:(j + 1) * 128] = (pr * wr - pi * wi).astype(BF16)
-                wave[k, pl.ds(SIDE + at, CH), j * 128:(j + 1) * 128] = (pr * wi + pi * wr).astype(BF16)
+                re, im = [], []
+                for h in range(2):
+                    wr, wi = w[2 * h][j], w[2 * h + 1][j]
+                    pr = probe[0, k, pl.ds(j * SIDE + h * HALF + at, CH), :]
+                    pi = probe[1, k, pl.ds(j * SIDE + h * HALF + at, CH), :]
+                    re.append(pr * wr - pi * wi)
+                    im.append(pr * wi + pi * wr)
+                cols = slice(j * 128, (j + 1) * 128)
+                wave[k, 0, pl.ds(at, CH), cols] = (re[0] + re[1]).astype(BF16)
+                wave[k, 0, pl.ds(HALF + at, CH), cols] = (im[0] + im[1]).astype(BF16)
+                wave[k, 1, pl.ds(at, CH), cols] = (re[0] - re[1]).astype(BF16)
+                wave[k, 1, pl.ds(HALF + at, CH), cols] = (im[0] - im[1]).astype(BF16)
         return power
 
-    power = lax.fori_loop(0, STEPS, make_exit, none, unroll=UNROLL)
+    power = lax.fori_loop(0, STEPS // 2, make_exit, none, unroll=UNROLL // 2)
     stats[0] = stats[0] + live * power
 
-    def transform(first, second):
-        for k in range(MODES):
-            res = jnp.dot(first[...], wave[k], preferred_element_type=F32).astype(BF16)
-            half[k * SIDE:(k + 1) * SIDE, 0:SIDE] = res[0:SIDE]
-            half[k * SIDE:(k + 1) * SIDE, SIDE:EXT] = res[SIDE:EXT]
-        field[...] = jnp.dot(half[...], second[...], preferred_element_type=F32)
-
-    transform(left_tab, right_tab)
+    for k in range(MODES):
+        for parity in range(2):
+            res = jnp.dot(tables[parity], wave[k, parity], preferred_element_type=F32)
+            spot = slice(k * SIDE + parity * HALF, k * SIDE + (parity + 1) * HALF)
+            for o in range(2):
+                near = res[o * HALF:(o + 1) * HALF, 0:HALF]
+                far = res[o * HALF:(o + 1) * HALF, HALF:SIDE]
+                half[0, spot, o * HALF:(o + 1) * HALF] = (near + far).astype(BF16)
+                half[1, spot, o * HALF:(o + 1) * HALF] = (near - far).astype(BF16)
+    for parity in range(2):
+        field[parity] = jnp.dot(half[parity], tables[4 + parity], preferred_element_type=F32)
 
     def correct(i, misfit):
         at = pl.multiple_of(i * CH, CH)
-        parts = [
-            (field[pl.ds(k * SIDE + at, CH), 0:SIDE], field[pl.ds(k * SIDE + at, CH), SIDE:EXT])
-            for k in range(MODES)
-        ]
-        total = sum(re * re + im * im for re, im in parts)
-        modulus = jnp.sqrt(total)
-        amplitude = mags[batch, slot, pl.ds(at, CH), :]
-        factor = live * (amplitude / jnp.maximum(modulus, floor_value) - 1.0)
-        gap = modulus - amplitude
-        gap = gap * gap
-        for k in range(MODES):
-            wave[k, pl.ds(at, CH), :] = (parts[k][0] * factor).astype(BF16)
-            wave[k, pl.ds(SIDE + at, CH), :] = (parts[k][1] * factor).astype(BF16)
-        return misfit + fold(gap[:, 0:128]) + fold(gap[:, 128:256])
+        parity = i // (STEPS // 2)
+        to = pl.multiple_of((i % (STEPS // 2)) * CH, CH)
+        for q in range(2):
+            parts = [
+                (field[q, pl.ds(k * SIDE + at, CH), 0:HALF], field[q, pl.ds(k * SIDE + at, CH), HALF:SIDE])
+                for k in range(MODES)
+            ]
+            total = sum(re * re + im * im for re, im in parts)
+            modulus = jnp.sqrt(total)
+            amplitude = mags[batch, slot, pl.ds(at, CH), q * HALF:(q + 1) * HALF]
+            factor = live * (amplitude / jnp.maximum(modulus, floor_value) - 1.0)
+            gap = modulus - amplitude
+            misfit = misfit + fold(gap * gap)
+            cols = slice(q * HALF, (q + 1) * HALF)
+            for k in range(MODES):
+                wave[k, parity, pl.ds(to, CH), cols] = (parts[k][0] * factor).astype(BF16)
+                wave[k, parity, pl.ds(HALF + to, CH), cols] = (parts[k][1] * factor).astype(BF16)
+        return misfit
 
     misfit = lax.fori_loop(0, STEPS, correct, none, unroll=UNROLL)
     stats[1] = stats[1] + live * misfit
-    transform(right_tab, left_tab)
+
+    for k in range(MODES):
+        even = jnp.dot(tables[2], wave[k, 0], preferred_element_type=F32)
+        odd = jnp.dot(tables[3], wave[k, 1], preferred_element_type=F32)
+        for h, value in enumerate(((even + odd).astype(BF16), (even - odd).astype(BF16))):
+            spot = slice(k * SIDE + h * HALF, k * SIDE + (h + 1) * HALF)
+            for o in range(2):
+                for q in range(2):
+                    half[q, spot, o * HALF:(o + 1) * HALF] = value[
+                        o * HALF:(o + 1) * HALF, q * HALF:(q + 1) * HALF
+                    ]
+    for parity in range(2):
+        field[parity] = jnp.dot(half[parity], tables[6 + parity], preferred_element_type=F32)
 
     def spread(i, c):
         at = pl.multiple_of(i * CH, CH)
@@ -148,8 +190,13 @@
             wi = win[1, j, pl.ds(at, CH), :]
             tr = ti = None
             for k in range(MODES):
-                ur = field[pl.ds(k * SIDE + at, CH), j * 128:(j + 1) * 128]
-                ui = field[pl.ds(k * SIDE + at, CH), SIDE + j * 128:SIDE + (j + 1) * 128]
+                source = pl.ds(k * SIDE + at, CH)
+                if j == 0:
+                    ur = field[0, source, 0:HALF] + field[1, source, 0:HALF]
+                    ui = field[0, source, HALF:SIDE] + field[1, source, HALF:SIDE]
+                else:
+                    ur = field[0, source, 0:HALF] - field[1, source, 0:HALF]
+                    ui = field[0, source, HALF:SIDE] - field[1, source, HALF:SIDE]
                 spot = pl.ds(j * SIDE + at, CH)
                 pr = probe[0, k, spot, :]
                 pi = probe[1, k, spot, :]
@@ -175,9 +222,9 @@
 
 
 def body(
-    rows_ref, cols_ref, counts_ref, object_in, probe_in, mags_in, left_in, right_in,
+    rows_ref, cols_ref, counts_ref, object_in, probe_in, mags_in, tables_in, sort_in,
     object_out, probe_out, errors,
-    obj, probes, grad, pgrad, terms, stats, mags, left_tab, right_tab, win, wave, half, field,
+    obj, probes, grad, pgrad, terms, stats, mags, tables, sort, win, wave, half, field,
     core_in, acc, one_in, one, two_in, z_in, tile_in, tile_z, tile_core,
     col_in, row_in, mid, rdma_send, rdma_recv, local, ready,
 ):
@@ -211,8 +258,8 @@
             probe_in.at[:, :, :, j * 128:(j + 1) * 128],
             probes.at[0, :, :, j * SIDE:(j + 1) * SIDE, :],
         )
-    load(left_in, left_tab)
-    load(right_in, right_tab)
+    load(tables_in, tables)
+    load(sort_in, sort)
     load(mags_in.at[0, 0], mags)
 
     count = [0]
@@ -289,6 +336,22 @@
 
     lax.fori_loop(0, 12, clear, 0)
     pgrad[...] = jnp.zeros_like(pgrad)
+    wait(loads[2:7])
+
+    def pieces(x):
+        high = x.astype(BF16)
+        rest = x - high.astype(F32)
+        middle = rest.astype(BF16)
+        return (high, middle, (rest - middle.astype(F32)).astype(BF16))
+
+    def arrange(n, c):
+        b, s = n // SLOTS, n % SLOTS
+        x = sum(jnp.dot(sort[0], v, preferred_element_type=F32) for v in pieces(mags[b, s]))
+        mags[b, s] = sum(jnp.dot(v, sort[1], preferred_element_type=F32) for v in pieces(x))
+        return c
+
+    lax.fori_loop(0, BATCHES * SLOTS, arrange, 0)
+
     halo = [halo_messages(p) for p in range(2)]
     for p in range(2):
         wait(first[p])
@@ -299,7 +362,6 @@
     for p in range(2):
         wait_halo(halo[p])
     greet(ready)
-    wait(loads[2:7])
 
     base = count[0]
 
@@ -312,7 +374,7 @@
 
         def one_slot(slot, c):
             visit(
-                batch, slot, rows_ref, cols_ref, counts_ref, obj, probe, mags, left_tab, right_tab,
+                batch, slot, rows_ref, cols_ref, counts_ref, obj, probe, mags, tables,
                 terms, pgrad, stats, win, wave, half, field,
             )
             return c
@@ -578,12 +640,12 @@
             pltpu.VMEM((SLOTS, 2, 5, 3 * SIDE, 128), F32),
             pltpu.VMEM((2, 8, 128), F32),
             pltpu.VMEM((BATCHES, SLOTS, SIDE, SIDE), F32),
-            pltpu.VMEM((EXT, EXT), BF16),
-            pltpu.VMEM((EXT, EXT), BF16),
+            pltpu.VMEM((8, SIDE, SIDE), BF16),
+            pltpu.VMEM((2, SIDE, SIDE), BF16),
             pltpu.VMEM((2, 2, SIDE, 128), F32),
-            pltpu.VMEM((MODES, EXT, SIDE), BF16),
-            pltpu.VMEM((MODES * SIDE, EXT), BF16),
-            pltpu.VMEM((MODES * SIDE, EXT), F32),
+            pltpu.VMEM((MODES, 2, SIDE, SIDE), BF16),
+            pltpu.VMEM((2, MODES * SIDE, SIDE), BF16),
+            pltpu.VMEM((2, MODES * SIDE, SIDE), F32),
             pltpu.VMEM((MODES, EXT, 128), F32),
             pltpu.VMEM((MODES, EXT, 128), F32),
             pltpu.VMEM((3, MODES, 128, 128), F32),

time: 292 us -> 281 us (0.962)
  Pallas kernels: 284 us -> 274 us
    pallas_call x1, Pallas kernels: 284 us -> 274 us  [on_device(): pl.pallas_call(body, out_shape=(jax.ShapeDtypeStruct((2, SIDE, SIDE), F32...]
where the time goes in v6:
time: 281 us
  Pallas kernels  274 us (98%)
  local copies, waits for them, and re-layouts  4.91 us (2%)
    pallas_call x1, Pallas kernels, on_device(): pl.pallas_call(body, out_shape=(jax.ShapeDtypeStruct((2, SIDE, SIDE), F32...  274 us

profile of v6, /device:TPU:1, one launch (start us, length us, event | category | flops | bytes accessed | tf_op | source)
XLA Modules:
  0.0 280.5 jit_solution(10936528359085030231)
XLA Ops:
  0.6 273.6 %whole_sweep.1 = (f32[2,256,256]{2,1,0:T(8,128)}, f32[2,4,256,256]{3,2,1,0:T(8,128)}, f32[4,8,128]{2,1,0:T(8,128)}) custom-call(s32[1,1,2,3]{3,2,1,0:T(2,128)} %rows_ref.1, s32[1,1,2,3]{3,2,1,0:T(2,128)} %cols_ref.1, s32[1,1,2]{2,1,0:T(1,128)} %counts_ref.1, f32[2,256,256]{2,1,0:T(8,128)} %object_in.1, f32[2,4,256,256]{3,2,1,0:T(8,128)} %probe_in.1, ...), custom_call_target="tpu_custom_call" | custom-call | flops 85899345920 | bytes 12582912 | tf_op jit(solution)/shard_map/whole_sweep/pallas_call | solution.py:626
  274.3 1.3 reduce_sum.9
  275.6 1.9 copy.13
  277.5 3.0 %copy.14 = f32[2,4,256,256]{3,2,1,0:T(8,128)} copy(f32[2,4,256,256]{3,2,1,0:T(8,128)} %get-tuple-element.13) | data formatting | bytes 4194304

commit v7 on v6

--- a/solution.py
+++ b/solution.py
@@ -226,13 +226,18 @@
     object_out, probe_out, errors,
     obj, probes, grad, pgrad, terms, stats, mags, tables, sort, win, wave, half, field,
     core_in, acc, one_in, one, two_in, z_in, tile_in, tile_z, tile_core,
-    col_in, row_in, mid, rdma_send, rdma_recv, local, ready,
+    inner_in, side_in, corner_in, row_in, rdma_send, rdma_recv, local, ready,
 ):
     row, col, core, coords, along, partner, tile = where_am_i()
     up, down = tile((row + 7) % 8, col), tile((row + 1) % 8, col)
-    left, right = tile(row, (col + 15) % 16), tile(row, (col + 1) % 16)
-    has_left, has_right, has_up, has_down = col > 0, col < 15, row > 0, row < 7
-    greeted = [partner, up, down, left, right]
+    beside = (col + 15 + 2 * core) % 16
+    outer = tile(row, beside)
+    outer_up, outer_down = tile((row + 7) % 8, beside), tile((row + 1) % 8, beside)
+    has_up, has_down = row > 0, row < 7
+    has_outer = jnp.where(core == 0, col > 0, col < 15)
+    inner_halo, outer_halo = 3 * (1 - core), 3 * core
+    inner_own, outer_own = 2 - core, 1 + core
+    greeted = [partner, outer, up, down, outer_up, outer_down]
     for axis in ("x", "y", "z"):
         for d in (1, 2, 3):
             greeted.append(along(axis, (coords[axis] + d) % 4))
@@ -241,6 +246,12 @@
         for peer in greeted:
             pl.semaphore_signal(sem, inc=1, device_id=peer, device_id_type=pl.DeviceIdType.MESH)
 
+    for p in range(2):
+        for b in (0, 3):
+            obj[p, b] = jnp.zeros((EXT, 128), F32)
+        for b in (1, 2):
+            obj[p, b, 0:HALF, :] = jnp.zeros((HALF, 128), F32)
+            obj[p, b, SIDE + HALF:EXT, :] = jnp.zeros((HALF, 128), F32)
     barrier = pltpu.get_barrier_semaphore()
     greet(barrier)
 
@@ -281,49 +292,56 @@
         for copy in copies:
             copy.wait()
 
-    def halo_messages(p):
-        return [
-            message(obj.at[p, 2], obj.at[p, 0], right),
-            message(obj.at[p, 1], obj.at[p, 3], left),
-        ]
-
-    def start_halo(pair):
-        @pl.when(has_right)
-        def _():
-            pair[0].start()
-
-        @pl.when(has_left)
-        def _():
-            pair[1].start()
-
-    def wait_halo(pair):
-        @pl.when(has_right)
-        def _():
-            pair[0].wait_send()
-            pair[1].wait_recv()
-
-        @pl.when(has_left)
-        def _():
-            pair[1].wait_send()
-            pair[0].wait_recv()
+    class Halo:
+        def __init__(self, p):
+            both = jnp.logical_and
+            own, top, low = slice(HALF, SIDE + HALF), slice(HALF, SIDE), slice(SIDE, SIDE + HALF)
+            above, below = slice(0, HALF), slice(SIDE + HALF, EXT)
+            there = 3 * (1 - core)
+            self.parts = [
+                (message(obj.at[p, 1:3, top, :], obj.at[p, 1:3, below, :], up), has_up, has_down),
+                (message(obj.at[p, 1:3, low, :], obj.at[p, 1:3, above, :], down), has_down, has_up),
+                (message(obj.at[p, outer_own, own, :], obj.at[p, there, own, :], outer), has_outer, has_outer),
+                (
+                    message(obj.at[p, outer_own, top, :], obj.at[p, there, below, :], outer_up),
+                    both(has_up, has_outer), both(has_down, has_outer),
+                ),
+                (
+                    message(obj.at[p, outer_own, low, :], obj.at[p, there, above, :], outer_down),
+                    both(has_down, has_outer), both(has_up, has_outer),
+                ),
+            ]
+            self.inner = message(obj.at[p, inner_own], obj.at[p, 3 * core], partner)
+
+        def start(self):
+            for copy, sends, _ in self.parts:
+                @pl.when(sends)
+                def _():
+                    copy.start()
+
+        def wait_some(self, parts):
+            for copy, sends, takes in parts:
+                @pl.when(sends)
+                def _():
+                    copy.wait_send()
+
+                @pl.when(takes)
+                def _():
+                    copy.wait_recv()
+
+        def turn(self):
+            self.wait_some(self.parts[0:2])
+            self.inner.start()
+
+        def finish(self):
+            self.wait_some(self.parts[2:])
+            self.inner.wait()
 
     pl.semaphore_wait(barrier, len(greeted))
     wait(loads[0:2])
-    first = [
-        [
-            send(obj.at[p, 1:3, HALF:SIDE, :], row_in.at[1, p, :, 0:HALF, :], up),
-            send(obj.at[p, 1:3, SIDE:SIDE + HALF, :], row_in.at[0, p, :, 0:HALF, :], down),
-        ]
-        for p in range(2)
-    ]
-
-    @pl.when(jnp.logical_not(has_left))
-    def _():
-        obj[:, 0] = jnp.zeros((2, EXT, 128), F32)
-
-    @pl.when(jnp.logical_not(has_right))
-    def _():
-        obj[:, 3] = jnp.zeros((2, EXT, 128), F32)
+    halo = [Halo(p) for p in range(2)]
+    for p in range(2):
+        halo[p].start()
 
     def clear(i, c):
         at = pl.multiple_of(i * 64, 64)
@@ -352,15 +370,10 @@
 
     lax.fori_loop(0, BATCHES * SLOTS, arrange, 0)
 
-    halo = [halo_messages(p) for p in range(2)]
     for p in range(2):
-        wait(first[p])
-        for j in range(2):
-            obj[p, 1 + j, 0:HALF, :] = jnp.where(has_up, row_in[0, p, j, 0:HALF, :], 0.0)
-            obj[p, 1 + j, SIDE + HALF:EXT, :] = jnp.where(has_down, row_in[1, p, j, 0:HALF, :], 0.0)
-        start_halo(halo[p])
+        halo[p].turn()
     for p in range(2):
-        wait_halo(halo[p])
+        halo[p].finish()
     greet(ready)
 
     base = count[0]
@@ -399,17 +412,21 @@
 
         pl.semaphore_wait(ready, len(greeted))
 
+        inner_sent, outer_sent = [], []
+        for p in range(2):
+            add_terms(p, inner_halo)
+            inner_sent.append(send(grad.at[p, inner_halo], inner_in.at[p], partner))
         core_sent = [
             send(stats, tile_core, partner),
             send(pgrad.at[1 - core], core_in, partner),
         ]
-        cols_sent = []
         for p in range(2):
-            add_terms(p, 3)
-            cols = [send(grad.at[p, 3], col_in.at[0, p], right)]
-            add_terms(p, 0)
-            cols.append(send(grad.at[p, 0], col_in.at[1, p], left))
-            cols_sent.append(cols)
+            add_terms(p, outer_halo)
+            outer_sent.append([
+                send(grad.at[p, outer_halo, HALF:SIDE + HALF, :], side_in.at[p], outer),
+                send(grad.at[p, outer_halo, 0:HALF, :], corner_in.at[p, HALF:SIDE, :], outer_up),
+                send(grad.at[p, outer_halo, SIDE + HALF:EXT, :], corner_in.at[p, 0:HALF, :], outer_down),
+            ])
 
         def scatter(phase, source, landing, length, tile_value):
             me = coords[ORDERS[0][phase]]
@@ -444,36 +461,13 @@
         def tile_total(phase):
             return (tile_in[phase, 0] + tile_in[phase, 1]) + (tile_in[phase, 2] + tile_in[phase, 3])
 
-        def send_rows(p, j):
-            outer = [
-                send(mid.at[p, j, 0:HALF, :], row_in.at[1, p, j, 0:HALF], up),
-                send(mid.at[p, j, SIDE + HALF:EXT, :], row_in.at[0, p, j, HALF:SIDE], down),
+        def send_rows(p):
+            inner_sent[p].wait()
+            grad[p, inner_own] = grad[p, inner_own] + inner_in[p]
+            return [
+                send(grad.at[p, 1:3, 0:HALF, :], row_in.at[p, :, HALF:SIDE, :], up),
+                send(grad.at[p, 1:3, SIDE + HALF:EXT, :], row_in.at[p, :, 0:HALF, :], down),
             ]
-            inner = [
-                message(mid.at[p, j, HALF:SIDE, :], row_in.at[1, p, j, HALF:SIDE], up),
-                message(mid.at[p, j, SIDE:SIDE + HALF, :], row_in.at[0, p, j, 0:HALF], down),
-            ]
-
-            @pl.when(u < UPDATES - 1)
-            def _():
-                inner[0].start()
-                inner[1].start()
-
-            return (outer, inner)
-
-        def wait_rows(pair):
-            for outer, inner in pair:
-                wait(outer)
-
-            @pl.when(u < UPDATES - 1)
-            def _():
-                for outer, inner in pair:
-                    wait(inner)
-
-        def make_mid(p):
-            wait(cols_sent[p])
-            mid[p, 0] = grad[p, 1] + jnp.where(has_left, col_in[0, p], 0.0)
-            mid[p, 1] = grad[p, 2] + jnp.where(has_right, col_in[1, p], 0.0)
 
         wait(core_sent)
         for k in range(MODES):
@@ -492,31 +486,30 @@
         best = lax.fori_loop(0, EXT // 16, peak_step, jnp.zeros((8, 128), F32), unroll=4)
         rate = object_rate / (jnp.max(best) + tiny_value)
 
-        def update_object(p, j):
-            upper = jnp.where(has_up, row_in[0, p, j], 0.0)
-            lower = jnp.where(has_down, row_in[1, p, j], 0.0)
-            top = mid[p, j, 0:SIDE, :] + upper
-            low = mid[p, j, SIDE:EXT, :] + lower
-            rate_up = jnp.where(has_up, rate, 0.0)
-            rate_down = jnp.where(has_down, rate, 0.0)
-            b = 1 + j
-            obj[p, b, 0:HALF, :] = obj[p, b, 0:HALF, :] + rate_up * top[0:HALF]
-            obj[p, b, HALF:SIDE, :] = obj[p, b, HALF:SIDE, :] + rate * top[HALF:SIDE]
-            obj[p, b, SIDE:SIDE + HALF, :] = obj[p, b, SIDE:SIDE + HALF, :] + rate * low[0:HALF]
-            obj[p, b, SIDE + HALF:EXT, :] = obj[p, b, SIDE + HALF:EXT, :] + rate_down * low[HALF:SIDE]
+        def finish_object(p):
+            wait(rows_sent[p] + outer_sent[p])
+            for h, has in ((0, has_up), (1, has_down)):
+                there = slice(h * HALF, (h + 1) * HALF)
+                here = slice((h + 1) * HALF, (h + 2) * HALF)
+                for b in (1, 2):
+                    total = grad[p, b, here, :] + jnp.where(has, row_in[p, b - 1, there, :], 0.0)
+                    side = side_in[p, there, :] + jnp.where(has, corner_in[p, there, :], 0.0)
+                    total = total + jnp.where(jnp.logical_and(has_outer, outer_own == b), side, 0.0)
+                    obj[p, b, here, :] = obj[p, b, here, :] + rate * total
+
+            @pl.when(u < UPDATES - 1)
+            def _():
+                halo[p].start()
 
         for p in range(2):
             add_terms(p, 1)
             add_terms(p, 2)
-        make_mid(0)
-        rows_sent = [send_rows(0, 0), send_rows(0, 1)]
+        rows_sent = [send_rows(p) for p in range(2)]
 
         wait(sent)
         for k, v in enumerate(gather_sum(0, acc, one_in, 128)):
             one[k] = v
         sent = scatter(1, one, two_in, 32, tile_total(0))
-
-        make_mid(1)
 
         wait(sent)
         z = coords["z"]
@@ -529,7 +522,9 @@
             sent.append(send(tile_z.at[z], tile_z.at[z], peer))
             sent.append(send(z_in.at[z], z_in.at[z], peer))
         pgrad[...] = jnp.zeros_like(pgrad)
-        rows_sent.append(send_rows(1, 0))
+        halo = [Halo(p) for p in range(2)]
+        for p in range(2):
+            finish_object(p)
         wait(sent)
 
         totals = (tile_z[0] + tile_z[1]) + (tile_z[2] + tile_z[3])
@@ -558,25 +553,17 @@
             return out
 
         out2 = spread(1, 32)
-        rows_sent.append(send_rows(1, 1))
-        halo = [halo_messages(p) for p in range(2)]
-
-        def finish_object(p):
-            wait_rows(rows_sent[2 * p:2 * p + 2])
-            for j in range(2):
-                update_object(p, j)
-
-            @pl.when(u < UPDATES - 1)
-            def _():
-                start_halo(halo[p])
-
         wait(out2.values())
         out1 = spread(0, 128)
-        finish_object(0)
         to_core = []
         for g in range(2):
             block = block_of(g, starts[g][0], 128)
             to_core.append(send(block, block, partner))
+
+        @pl.when(u < UPDATES - 1)
+        def _():
+            for p in range(2):
+                halo[p].turn()
 
         for d in (1, 3, 2):
             for g in range(2):
@@ -585,13 +572,12 @@
                 block = block_of(g, (coords[axis] + 4 - d) % 4 * 128, 128)
                 to_core.append(send(block, block, partner))
 
-        finish_object(1)
         wait(to_core)
 
         @pl.when(u < UPDATES - 1)
         def _():
             for p in range(2):
-                wait_halo(halo[p])
+                halo[p].finish()
             greet(ready)
 
         return carry
@@ -655,9 +641,10 @@
             pltpu.VMEM((2, 4, 2, 8, 128), F32),
             pltpu.VMEM((4, 2, 8, 128), F32),
             pltpu.VMEM((2, 8, 128), F32),
-            pltpu.VMEM((2, 2, EXT, 128), F32),
-            pltpu.VMEM((2, 2, 2, SIDE, 128), F32),
-            pltpu.VMEM((2, 2, EXT, 128), F32),
+            pltpu.VMEM((2, EXT, 128), F32),
+            pltpu.VMEM((2, SIDE, 128), F32),
+            pltpu.VMEM((2, SIDE, 128), F32),
+            pltpu.VMEM((2, 2, SIDE, 128), F32),
             pltpu.SemaphoreType.DMA((messages,)),
             pltpu.SemaphoreType.DMA((messages,)),
             pltpu.SemaphoreType.DMA((8,)),

time: 281 us -> 262 us (0.932)
  Pallas kernels: 274 us -> 255 us
    pallas_call x1, Pallas kernels: 274 us -> 255 us  [on_device(): pl.pallas_call(body, out_shape=(jax.ShapeDtypeStruct((2, SIDE, SIDE), F32...]
where the time goes in v7:
time: 262 us
  Pallas kernels  255 us (97%)
  local copies, waits for them, and re-layouts  4.91 us (2%)
    pallas_call x1, Pallas kernels, on_device(): pl.pallas_call(body, out_shape=(jax.ShapeDtypeStruct((2, SIDE, SIDE), F32...  255 us

profile of v7, /device:TPU:1, one launch (start us, length us, event | category | flops | bytes accessed | tf_op | source)
XLA Modules:
  0.0 261.6 jit_solution(5974277242323898886)
XLA Ops:
  0.6 254.7 %whole_sweep.1 = (f32[2,256,256]{2,1,0:T(8,128)}, f32[2,4,256,256]{3,2,1,0:T(8,128)}, f32[4,8,128]{2,1,0:T(8,128)}) custom-call(s32[1,1,2,3]{3,2,1,0:T(2,128)} %rows_ref.1, s32[1,1,2,3]{3,2,1,0:T(2,128)} %cols_ref.1, s32[1,1,2]{2,1,0:T(1,128)} %counts_ref.1, f32[2,256,256]{2,1,0:T(8,128)} %object_in.1, f32[2,4,256,256]{3,2,1,0:T(8,128)} %probe_in.1, ...), custom_call_target="tpu_custom_call" | custom-call | flops 85899345920 | bytes 12582912 | tf_op jit(solution)/shard_map/whole_sweep/pallas_call | solution.py:612
  255.3 1.3 reduce_sum.9
  256.7 1.9 copy.13
  258.5 3.0 %copy.14 = f32[2,4,256,256]{3,2,1,0:T(8,128)} copy(f32[2,4,256,256]{3,2,1,0:T(8,128)} %get-tuple-element.13) | data formatting | bytes 4194304

commit v8 on v7

--- a/solution.py
+++ b/solution.py
@@ -413,13 +413,13 @@
         pl.semaphore_wait(ready, len(greeted))
 
         inner_sent, outer_sent = [], []
-        for p in range(2):
-            add_terms(p, inner_halo)
-            inner_sent.append(send(grad.at[p, inner_halo], inner_in.at[p], partner))
         core_sent = [
             send(stats, tile_core, partner),
             send(pgrad.at[1 - core], core_in, partner),
         ]
+        for p in range(2):
+            add_terms(p, inner_halo)
+            inner_sent.append(send(grad.at[p, inner_halo], inner_in.at[p], partner))
         for p in range(2):
             add_terms(p, outer_halo)
             outer_sent.append([
@@ -523,8 +523,6 @@
             sent.append(send(z_in.at[z], z_in.at[z], peer))
         pgrad[...] = jnp.zeros_like(pgrad)
         halo = [Halo(p) for p in range(2)]
-        for p in range(2):
-            finish_object(p)
         wait(sent)
 
         totals = (tile_z[0] + tile_z[1]) + (tile_z[2] + tile_z[3])
@@ -553,8 +551,10 @@
             return out
 
         out2 = spread(1, 32)
+        finish_object(0)
         wait(out2.values())
         out1 = spread(0, 128)
+        finish_object(1)
         to_core = []
         for g in range(2):
             block = block_of(g, starts[g][0], 128)

time: 262 us -> 255 us (0.973)
  Pallas kernels: 255 us -> 247 us
    pallas_call x1, Pallas kernels: 255 us -> 247 us  [on_device(): pl.pallas_call(body, out_shape=(jax.ShapeDtypeStruct((2, SIDE, SIDE), F32...]
where the time goes in v8:
time: 255 us; the launch traced here: 254 us
  Pallas kernels  247 us (97%)
  local copies, waits for them, and re-layouts  4.91 us (2%)
    pallas_call x1, Pallas kernels, on_device(): pl.pallas_call(body, out_shape=(jax.ShapeDtypeStruct((2, SIDE, SIDE), F32...  247 us

profile of v8, /device:TPU:1, one launch (start us, length us, event | category | flops | bytes accessed | tf_op | source)
XLA Modules:
  0.0 254.1 jit_solution(1127126576569695307)
XLA Ops:
  0.6 247.2 %whole_sweep.1 = (f32[2,256,256]{2,1,0:T(8,128)}, f32[2,4,256,256]{3,2,1,0:T(8,128)}, f32[4,8,128]{2,1,0:T(8,128)}) custom-call(s32[1,1,2,3]{3,2,1,0:T(2,128)} %rows_ref.1, s32[1,1,2,3]{3,2,1,0:T(2,128)} %cols_ref.1, s32[1,1,2]{2,1,0:T(1,128)} %counts_ref.1, f32[2,256,256]{2,1,0:T(8,128)} %object_in.1, f32[2,4,256,256]{3,2,1,0:T(8,128)} %probe_in.1, ...), custom_call_target="tpu_custom_call" | custom-call | flops 85899345920 | bytes 12582912 | tf_op jit(solution)/shard_map/whole_sweep/pallas_call | solution.py:612
  247.9 1.3 reduce_sum.9
  249.2 1.9 copy.13
  251.1 3.0 %copy.14 = f32[2,4,256,256]{3,2,1,0:T(8,128)} copy(f32[2,4,256,256]{3,2,1,0:T(8,128)} %get-tuple-element.13) | data formatting | bytes 4194304

commit v9 on v8

--- a/solution.py
+++ b/solution.py
@@ -75,7 +75,7 @@
 ORDERS = (("x", "y", "z"), ("y", "x", "z"))
 CH = 16
 STEPS = SIDE // CH
-UNROLL = 4
+UNROLL = 8
 
 
 def fold(x):
@@ -415,7 +415,8 @@
         inner_sent, outer_sent = [], []
         core_sent = [
             send(stats, tile_core, partner),
-            send(pgrad.at[1 - core], core_in, partner),
+            send(pgrad.at[1 - core, 0:2], core_in.at[0:2], partner),
+            send(pgrad.at[1 - core, 2:4], core_in.at[2:4], partner),
         ]
         for p in range(2):
             add_terms(p, inner_halo)
@@ -428,14 +429,16 @@
                 send(grad.at[p, outer_halo, SIDE + HALF:EXT, :], corner_in.at[p, 0:HALF, :], outer_down),
             ])
 
-        def scatter(phase, source, landing, length, tile_value):
+        def scatter(phase, source, landing, length, tile_value, groups=(0, 1)):
             me = coords[ORDERS[0][phase]]
-            tile_in[phase, me] = tile_value
             slot = tile_in.at[phase, me]
+            if tile_value is not None:
+                tile_in[phase, me] = tile_value
             sent = []
             for d in (2, 1, 3):
-                sent.append(send(slot, slot, along(ORDERS[0][phase], (me + d) % 4)))
-                for g in range(2):
+                if tile_value is not None:
+                    sent.append(send(slot, slot, along(ORDERS[0][phase], (me + d) % 4)))
+                for g in groups:
                     axis = ORDERS[g][phase]
                     to = (coords[axis] + d) % 4
                     at = pl.multiple_of(to * length, length)
@@ -469,10 +472,14 @@
                 send(grad.at[p, 1:3, SIDE + HALF:EXT, :], row_in.at[p, :, 0:HALF, :], down),
             ]
 
-        wait(core_sent)
-        for k in range(MODES):
+        wait(core_sent[0:2])
+        for k in (0, 1):
             acc[k] = pgrad[core, k] + core_in[k]
-        sent = scatter(0, acc, one_in, 128, stats[...] + tile_core[...])
+        sent = scatter(0, acc, one_in, 128, stats[...] + tile_core[...], (0,))
+        wait(core_sent[2:3])
+        for k in (2, 3):
+            acc[k] = pgrad[core, k] + core_in[k]
+        sent += scatter(0, acc, one_in, 128, None, (1,))
 
         def peak_step(i, best):
             at = pl.multiple_of(i * 16, 16)

time: 255 us -> 251 us (0.984)
  Pallas kernels: 247 us -> 243 us
    pallas_call x1, Pallas kernels: 247 us -> 243 us  [on_device(): pl.pallas_call(body, out_shape=(jax.ShapeDtypeStruct((2, SIDE, SIDE), F32...]
where the time goes in v9:
time: 251 us; the launch traced here: 250 us
  Pallas kernels  243 us (97%)
  local copies, waits for them, and re-layouts  4.91 us (2%)
    pallas_call x1, Pallas kernels, on_device(): pl.pallas_call(body, out_shape=(jax.ShapeDtypeStruct((2, SIDE, SIDE), F32...  243 us

profile of v9, /device:TPU:1, one launch (start us, length us, event | category | flops | bytes accessed | tf_op | source)
XLA Modules:
  0.0 250.4 jit_solution(13720654103445109668)
XLA Ops:
  0.6 243.5 %whole_sweep.1 = (f32[2,256,256]{2,1,0:T(8,128)}, f32[2,4,256,256]{3,2,1,0:T(8,128)}, f32[4,8,128]{2,1,0:T(8,128)}) custom-call(s32[1,1,2,3]{3,2,1,0:T(2,128)} %rows_ref.1, s32[1,1,2,3]{3,2,1,0:T(2,128)} %cols_ref.1, s32[1,1,2]{2,1,0:T(1,128)} %counts_ref.1, f32[2,256,256]{2,1,0:T(8,128)} %object_in.1, f32[2,4,256,256]{3,2,1,0:T(8,128)} %probe_in.1, ...), custom_call_target="tpu_custom_call" | custom-call | flops 85899345920 | bytes 12582912 | tf_op jit(solution)/shard_map/whole_sweep/pallas_call | solution.py:619
  244.1 1.3 reduce_sum.9
  245.4 1.9 copy.13
  247.3 3.0 %copy.14 = f32[2,4,256,256]{3,2,1,0:T(8,128)} copy(f32[2,4,256,256]{3,2,1,0:T(8,128)} %get-tuple-element.13) | data formatting | bytes 4194304

commit v10 on v9

--- a/solution.py
+++ b/solution.py
@@ -75,7 +75,7 @@
 ORDERS = (("x", "y", "z"), ("y", "x", "z"))
 CH = 16
 STEPS = SIDE // CH
-UNROLL = 8
+UNROLL = 16
 
 
 def fold(x):

time: 251 us -> 241 us (0.960)
  Pallas kernels: 243 us -> 234 us
    pallas_call x1, Pallas kernels: 243 us -> 234 us  [on_device(): pl.pallas_call(body, out_shape=(jax.ShapeDtypeStruct((2, SIDE, SIDE), F32...]
where the time goes in v10:
time: 241 us
  Pallas kernels  234 us (97%)
  local copies, waits for them, and re-layouts  4.91 us (2%)
    pallas_call x1, Pallas kernels, on_device(): pl.pallas_call(body, out_shape=(jax.ShapeDtypeStruct((2, SIDE, SIDE), F32...  234 us
    unnamed x2, local copies, waits for them, and re-layouts  4.91 us

profile of v10, /device:TPU:1, one launch (start us, length us, event | category | flops | bytes accessed | tf_op | source)
XLA Modules:
  0.0 241.0 jit_solution(16344485224024978166)
XLA Ops:
  0.6 234.1 %whole_sweep.1 = (f32[2,256,256]{2,1,0:T(8,128)}, f32[2,4,256,256]{3,2,1,0:T(8,128)}, f32[4,8,128]{2,1,0:T(8,128)}) custom-call(s32[1,1,2,3]{3,2,1,0:T(2,128)} %rows_ref.1, s32[1,1,2,3]{3,2,1,0:T(2,128)} %cols_ref.1, s32[1,1,2]{2,1,0:T(1,128)} %counts_ref.1, f32[2,256,256]{2,1,0:T(8,128)} %object_in.1, f32[2,4,256,256]{3,2,1,0:T(8,128)} %probe_in.1, ...), custom_call_target="tpu_custom_call" | custom-call | flops 85899345920 | bytes 12582912 | tf_op jit(solution)/shard_map/whole_sweep/pallas_call | solution.py:619
  234.7 1.3 reduce_sum.9
  236.1 1.9 copy.13
  237.9 3.0 %copy.14 = f32[2,4,256,256]{3,2,1,0:T(8,128)} copy(f32[2,4,256,256]{3,2,1,0:T(8,128)} %get-tuple-element.13) | data formatting | bytes 4194304
